TPU v7x, 256 devices: a whole 4x4x8 slice. The times are simulated.
256 devices in a mesh: band: 16 (over y_lo, z), grid: 16 (over x, y_hi, core).
Axes of the slice: x: 4, y: 4 (y_hi: 2, y_lo: 2; y = y_hi * 2 + y_lo), z: 8, core: 2. Of those that a mesh axis runs over, the one named last changes fastest.
Arguments:
- bands: bfloat16 [2, 32, 128, 128, 128], P(None, 'band', 'grid'), may hold values from -6 to 6
- occupations: float32 [32], P('band'), may hold values from 0.25 to 1
- external: float32 [128, 128, 128], P('grid'), may hold values from 0 to 2
- density_in: float32 [128, 128, 128], P('grid'), may hold values from -0.2 to 1.4
- prev_density: float32 [128, 128, 128], P('grid'), may hold values from 0 to 1.2
- prev_residual: float32 [128, 128, 128], P('grid'), may hold values from -1.3 to 0.3
- hist_density: float32 [5, 128, 128, 128], P(None, 'grid'), may hold values from 0 to 1
- hist_residual: float32 [5, 128, 128, 128], P(None, 'grid'), may hold values from -0.6 to 1
Outputs:
- density: float32 [128, 128, 128], P('grid')
- residual: float32 [128, 128, 128], P('grid')
All inputs are finite; a program needn't handle non-finite values.
Results may differ from a plain program's by a relative error of at most 0.018.
The roundings to bfloat16 on the way count: a program that leaves them out, or rounds other values in their place, can miss the bound.
Values may be sent and summed in bfloat16 or wider, within the bound.
A program may use at most 128 MiB of HBM per device.

v0:
```python
import math

import jax
import jax.numpy as jnp
from jax import lax
from jax.sharding import PartitionSpec as P

NG = 128
DEPTH = 6
ITERS = 3


time_step = 0.25
energy_shift = 2.5
coupling = 1.0
mixing_weight = 0.5
ridge_share = 0.1
ridge_floor = 0.01
density_scale = 8.0
highest = lax.Precision.HIGHEST


def sent_to_all(array, axis):
    count = lax.axis_size(axis)
    return lax.all_to_all(
        jnp.broadcast_to(array[None], (count, *array.shape)), axis, 0, 0, tiled=True
    )


def of_everyone(array, axis):
    return sent_to_all(array, axis).sum(axis=0)


def over_pieces(array, axis):
    blocks = lax.all_gather(array, axis).astype(jnp.float32)
    return blocks.sum(axis=0)


def fourier_tables(length, frequency):
    positions = jnp.arange(length, dtype=jnp.int32)
    phase_index = positions[:, None] * frequency[None, :] % length
    angles = phase_index.astype(jnp.float32) * (2.0 * math.pi / length)
    unit_scale = 1.0 / math.sqrt(length)
    return (
        (jnp.cos(angles) * unit_scale).astype(jnp.bfloat16),
        (jnp.sin(angles) * unit_scale).astype(jnp.bfloat16),
    )


def complex_block(cosine_part, sine_part, orientation):
    sine_signed = sine_part * orientation
    upper_half = jnp.concatenate([cosine_part, sine_signed], axis=1)
    lower_half = jnp.concatenate([-sine_signed, cosine_part], axis=1)
    return jnp.concatenate([upper_half, lower_half], axis=0)


def solve_definite(matrix, vector):
    extent = matrix.shape[0]
    factor_low = jnp.zeros_like(matrix)
    for column in range(extent):
        pivot_value = jnp.sqrt(
            matrix[column, column]
            - jnp.sum(factor_low[column, :column] * factor_low[column, :column])
        )
        factor_low = factor_low.at[column, column].set(pivot_value)
        for row_index in range(column + 1, extent):
            element = (
                matrix[row_index, column]
                - jnp.sum(factor_low[row_index, :column] * factor_low[column, :column])
            ) / pivot_value
            factor_low = factor_low.at[row_index, column].set(element)
    middle = jnp.zeros_like(vector)
    for row_index in range(extent):
        element = (
            vector[row_index] - jnp.sum(factor_low[row_index, :row_index] * middle[:row_index])
        ) / factor_low[row_index, row_index]
        middle = middle.at[row_index].set(element)
    result = jnp.zeros_like(vector)
    for row_index in reversed(range(extent)):
        element = (
            middle[row_index]
            - jnp.sum(factor_low[row_index + 1 :, row_index] * result[row_index + 1 :])
        ) / factor_low[row_index, row_index]
        result = result.at[row_index].set(element)
    return result


def local(
    bands,
    occupations,
    external,
    density_in,
    prev_density,
    prev_residual,
    hist_density,
    hist_residual,
):
    grid_count = lax.axis_size("grid")
    band_count = lax.axis_size("band")
    slab_planes = external.shape[0]
    cells_total = NG * NG * NG
    bands_total = occupations.shape[0] * band_count
    frequency = jnp.arange(-(NG // 4), NG // 4, dtype=jnp.int32)
    kept_count = frequency.shape[0]
    inside = ((frequency >= -(NG // 4)) & (frequency < NG // 4)).astype(jnp.float32)
    cosine_part, sine_part = fourier_tables(NG, frequency)
    forward_block = complex_block(cosine_part, sine_part, -1.0)
    inverse_block = complex_block(cosine_part.T, sine_part.T, 1.0)
    forward_axis = forward_block.reshape(2, NG, 2, kept_count)
    inverse_axis = inverse_block.reshape(2, kept_count, 2, NG)
    column_rows = kept_count // grid_count
    column_start = lax.axis_index("grid") * column_rows
    local_freq = lax.dynamic_slice_in_dim(frequency, column_start, column_rows).astype(jnp.float32)
    local_inside = lax.dynamic_slice_in_dim(inside, column_start, column_rows)
    squared = frequency.astype(jnp.float32) * frequency.astype(jnp.float32)
    quarter = NG / 4.0
    radius = (
        squared[None, :, None] + (local_freq * local_freq)[:, None, None] + squared[None, None, :]
    )
    kinetic = jnp.exp(-time_step * radius / (quarter * quarter))
    kinetic = kinetic * local_inside[:, None, None] * inside[None, :, None] * inside[None, None, :]
    history_flat = hist_residual.reshape(DEPTH - 1, -1)
    gram_kept = of_everyone(
        jnp.dot(history_flat, history_flat.T, precision=highest) / cells_total, "grid"
    )
    orbitals = jnp.concatenate([bands[0], bands[1]], axis=-1)
    density_now = density_in
    density_prev = prev_density
    residual_prev = prev_residual
    density_diffs = hist_density
    residual_diffs = hist_residual
    residual = density_in
    for iteration in range(ITERS):
        factor = jnp.exp(-time_step * (external + coupling * density_now - energy_shift))
        doubled = jnp.concatenate([factor, factor], axis=-1)
        weighted = (orbitals.astype(jnp.float32) * doubled).astype(jnp.bfloat16)
        band_items = orbitals.shape[0]
        along_z = jnp.dot(weighted, forward_block, preferred_element_type=jnp.float32).astype(
            jnp.bfloat16
        )
        split_z = along_z.reshape(band_items, slab_planes, NG, 2, kept_count)
        along_y = jnp.einsum(
            "bxycz,cydk->bkxdz", split_z, forward_axis, preferred_element_type=jnp.float32
        )
        along_y = along_y.astype(jnp.bfloat16).reshape(
            band_items, kept_count, slab_planes, 2 * kept_count
        )
        exchanged = lax.all_to_all(along_y, "grid", split_axis=1, concat_axis=2, tiled=True)
        item_count = exchanged.shape[0]
        spread = exchanged.reshape(item_count, column_rows, NG, 2, kept_count)
        spectral = jnp.einsum(
            "byxcz,cxdk->bykdz", spread, forward_axis, preferred_element_type=jnp.float32
        )
        damped = (spectral * kinetic[None, :, :, None, :]).astype(jnp.bfloat16)
        spatial = jnp.einsum(
            "bykdz,dkcx->byxcz", damped, inverse_axis, preferred_element_type=jnp.float32
        )
        returned = lax.all_to_all(
            spatial.astype(jnp.bfloat16).reshape(item_count, column_rows, NG, 2 * kept_count),
            "grid",
            split_axis=2,
            concat_axis=1,
            tiled=True,
        )
        split_back = returned.reshape(band_items, kept_count, slab_planes, 2, kept_count)
        back_y = jnp.einsum(
            "bkxdz,dkcy->bxycz", split_back, inverse_axis, preferred_element_type=jnp.float32
        )
        back_y = back_y.astype(jnp.bfloat16).reshape(band_items, slab_planes, NG, 2 * kept_count)
        orbitals = jnp.dot(back_y, inverse_block, preferred_element_type=jnp.float32).astype(
            jnp.bfloat16
        )
        real_part = orbitals[..., :NG].astype(jnp.float32)
        imag_part = orbitals[..., NG:].astype(jnp.float32)
        weighted_sq = occupations[:, None, None, None] * (
            real_part * real_part + imag_part * imag_part
        )
        density_out = over_pieces(
            (jnp.sum(weighted_sq, axis=0) * (density_scale / bands_total)).astype(jnp.bfloat16),
            "band",
        ).astype(jnp.float32)
        mixing_density_diffs = density_diffs
        mixing_residual_diffs = residual_diffs
        mixing_residual = density_out - density_now
        newest = mixing_residual - residual_prev
        mixing_density_diffs = jnp.concatenate(
            [
                mixing_density_diffs[mixing_density_diffs.shape[0] - (DEPTH - 1) :],
                (density_now - density_prev)[None],
            ],
            axis=0,
        )
        mixing_residual_diffs = jnp.concatenate(
            [mixing_residual_diffs[mixing_residual_diffs.shape[0] - (DEPTH - 1) :], newest[None]],
            axis=0,
        )
        flat_diffs = mixing_residual_diffs.reshape(DEPTH, -1)
        border_local = jnp.dot(flat_diffs, newest.reshape(-1), precision=highest) / cells_total
        right_local = (
            jnp.dot(flat_diffs, mixing_residual.reshape(-1), precision=highest) / cells_total
        )
        border, right_side = jax.tree.map(
            lambda part: of_everyone(part, "grid"), (border_local, right_local)
        )
        gram_matrix = (
            jnp.zeros((DEPTH, DEPTH), jnp.float32).at[: DEPTH - 1, : DEPTH - 1].set(gram_kept)
        )
        gram_matrix = gram_matrix.at[DEPTH - 1, :].set(border).at[:, DEPTH - 1].set(border)
        ridge_value = ridge_share * jnp.trace(gram_matrix) / DEPTH + ridge_floor
        coeffs = solve_definite(
            gram_matrix + ridge_value * jnp.eye(DEPTH, dtype=jnp.float32), right_side
        )
        combined = mixing_density_diffs + mixing_weight * mixing_residual_diffs
        density_next = (
            density_now
            + mixing_weight * mixing_residual
            - jnp.einsum("j,jxyz->xyz", coeffs, combined, precision=highest)
        )
        density_next, residual, density_diffs, residual_diffs, gram_kept = (
            density_next,
            mixing_residual,
            mixing_density_diffs,
            mixing_residual_diffs,
            gram_matrix[1:, 1:],
        )
        density_prev = density_now
        residual_prev = residual
        density_now = density_next
    return (density_now, residual)


def solution(mesh):
    placed = (
        P(None, "band", "grid", None, None),
        P("band"),
        P("grid", None, None),
        P("grid", None, None),
        P("grid", None, None),
        P("grid", None, None),
        P(None, "grid", None, None),
        P(None, "grid", None, None),
    )
    return jax.shard_map(
        local,
        mesh=mesh,
        in_specs=placed,
        out_specs=(P("grid", None, None), P("grid", None, None)),
        check_vma=False,
    )
```

profile of v0, /device:TPU:1, one launch (start us, length us, event | category | flops | bytes accessed | tf_op | source)
XLA Modules:
  0.0 699.8 jit_solution(16864654999003084204)
XLA Ops:
  12.7 8.4 %all-to-all-start = ((bf16[2,64,8,128]{3,2,0,1:T(8,128)(2,1)}), bf16[2,64,8,128]{3,2,0,1:T(8,128)(2,1)S(1)}, u32[]{:S(2)}, u32[]{:S(2)}) async-start(bf16[2,64,8,128]{3,2,0,1:T(8,128)(2,1)} %reshape.3028), calls=%async_computation | async-start | bytes 524288 | tf_op jit(solution)/shard_map/all_to_all | solution.py:148
  22.0 8.0 %all-to-all-done = bf16[2,64,8,128]{3,2,0,1:T(8,128)(2,1)S(1)} async-done(((bf16[2,64,8,128]{3,2,0,1:T(8,128)(2,1)}), bf16[2,64,8,128]{3,2,0,1:T(8,128)(2,1)S(1)}, u32[]{:S(2)}, u32[]{:S(2)}) %all-to-all-start) | async-done | bytes 262176 | tf_op jit(solution)/shard_map/all_to_all | solution.py:148
  31.0 12.3 %all_to_all.131 = bf16[2,4,128,128]{3,1,0,2:T(4,128)(2,1)S(1)} all-to-all(bf16[2,4,128,128]{3,1,0,2:T(4,128)(2,1)S(1)} %copy.284), channel_id=1, replica_groups=mesh['band'=16,'grid'=16] {'grid'}, dimensions={2} | all-to-all | bytes 524288 | tf_op jit(solution)/shard_map/all_to_all | solution.py:158
  47.2 9.5 %fusion.56 = f32[5,5]{1,0:T(8,128)S(1)} fusion(f32[5,8,128,128]{3,2,1,0:T(8,128)S(1)} %copy-done), kind=kOutput, calls=%fused_computation.92 | convolution fusion | flops 39321624 | bytes 2621540 | tf_op jit(solution)/shard_map/dot_general | solution.py:124
  56.7 11.0 %all_to_all.132 = f32[16,5,5]{2,1,0:T(8,128)S(1)} all-to-all(f32[16,5,5]{2,1,0:T(8,128)S(1)} %broadcast_in_dim.32), channel_id=1, replica_groups=mesh['band'=16,'grid'=16] {'grid'}, dimensions={0} | all-to-all | bytes 3200 | tf_op jit(solution)/shard_map/all_to_all | solution.py:25
  67.8 44.5 %all-gather.7.cloned.1.call-done = bf16[128,128,128]{2,1,0:T(8,128)(2,1)} async-done(((bf16[8,128,128]{2,1,0:T(8,128)(2,1)}), bf16[128,128,128]{2,1,0:T(8,128)(2,1)}) %all-gather.7.cloned.1.call-update) | async-done | bytes 4194320 | tf_op jit(solution)/shard_map/all_gather | solution.py:35
  118.8 9.8 %fusion.89 = f32[6]{0:T(128)S(1)} fusion(f32[8,128,128,1]{2,3,1,0:T(1,128)S(1)} %bitcast.561, f32[6,8,128,128]{3,2,1,0:T(8,128)S(1)} %get-tuple-element.1318), kind=kOutput, calls=%fused_computation.103 | convolution fusion | flops 9437190 | bytes 3670040 | tf_op jit(solution)/shard_map/dot_general | solution.py:198
  129.2 17.0 %all-to-all-start.4 = ((f32[16,1,6]{2,1,0:T(1,128)}), f32[16,1,6]{2,1,0:T(1,128)S(1)}, u32[]{:S(2)}, u32[]{:S(2)}) async-start(f32[16,1,6]{2,1,0:T(1,128)} %broadcast_in_dim.33), calls=%async_computation.4 | async-start | bytes 16384 | tf_op jit(solution)/shard_map/all_to_all | solution.py:25
  146.2 10.8 %fusion.92 = f32[6]{0:T(128)S(1)} fusion(f32[8,128,128,1]{2,3,1,0:T(1,128)} %bitcast.559, f32[6,8,128,128]{3,2,1,0:T(8,128)S(1)} %get-tuple-element.1318), kind=kOutput, calls=%fused_computation.104 | convolution fusion | flops 9437190 | bytes 3670040 | tf_op jit(solution)/shard_map/dot_general | solution.py:200
  157.7 7.2 %all-to-all-start.2 = ((f32[16,1,6]{2,1,0:T(1,128)}), f32[16,1,6]{2,1,0:T(1,128)S(1)}, u32[]{:S(2)}, u32[]{:S(2)}) async-start(f32[16,1,6]{2,1,0:T(1,128)} %broadcast_in_dim.31), calls=%async_computation.2 | async-start | bytes 16384 | tf_op jit(solution)/shard_map/all_to_all | solution.py:25
  167.6 4.3 all-to-all-done.2
  235.4 7.5 %fusion.16 = f32[1,8,128,128]{3,0,2,1:T(1,128)S(1)} fusion(f32[6,8,128,128]{3,2,1,0:T(8,128)} %get-tuple-element.1319, f32[6]{0:T(128)S(1)} %constant_dynamic-update-slice_fusion.26), kind=kOutput, calls=%fused_computation.27 | convolution fusion | flops 9437184 | bytes 3670040 | tf_op jit(solution)/shard_map/j,jxyz->xyz/dot_general | solution.py:217
  246.0 12.0 %all_to_all.133 = bf16[2,64,8,128]{3,2,0,1:T(8,128)(2,1)S(1)} all-to-all(bf16[2,64,8,128]{3,2,0,1:T(8,128)(2,1)S(1)} %reshape.3029), channel_id=1, replica_groups=mesh['band'=16,'grid'=16] {'grid'}, dimensions={1} | all-to-all | bytes 524288 | tf_op jit(solution)/shard_map/all_to_all | solution.py:148
  259.0 11.9 %all_to_all.134 = bf16[2,4,128,128]{3,1,0,2:T(4,128)(2,1)S(1)} all-to-all(bf16[2,4,128,128]{3,1,0,2:T(4,128)(2,1)S(1)} %copy.306), channel_id=1, replica_groups=mesh['band'=16,'grid'=16] {'grid'}, dimensions={2} | all-to-all | bytes 524288 | tf_op jit(solution)/shard_map/all_to_all | solution.py:158
  281.4 56.3 %all-gather.9.cloned.1.call-done = bf16[128,128,128]{2,1,0:T(8,128)(2,1)} async-done(((bf16[8,128,128]{2,1,0:T(8,128)(2,1)}), bf16[128,128,128]{2,1,0:T(8,128)(2,1)}) %all-gather.9.cloned.1.call-update) | async-done | bytes 4194320 | tf_op jit(solution)/shard_map/all_gather | solution.py:35
  337.7 3.2 convert_reduce_fusion.1
  344.2 9.8 %fusion.83 = f32[6]{0:T(128)S(1)} fusion(f32[8,128,128,1]{2,3,1,0:T(1,128)S(1)} %bitcast.556, f32[6,8,128,128]{3,2,1,0:T(8,128)S(1)} %get-tuple-element.1316), kind=kOutput, calls=%fused_computation.101 | convolution fusion | flops 9437190 | bytes 3670040 | tf_op jit(solution)/shard_map/dot_general | solution.py:198
  354.6 17.0 %all-to-all-start.8 = ((f32[16,1,6]{2,1,0:T(1,128)}), f32[16,1,6]{2,1,0:T(1,128)S(1)}, u32[]{:S(2)}, u32[]{:S(2)}) async-start(f32[16,1,6]{2,1,0:T(1,128)} %broadcast_in_dim.37), calls=%async_computation.8 | async-start | bytes 16384 | tf_op jit(solution)/shard_map/all_to_all | solution.py:25
  371.6 10.8 %fusion.86 = f32[6]{0:T(128)S(1)} fusion(f32[8,128,128,1]{2,3,1,0:T(1,128)} %bitcast.558, f32[6,8,128,128]{3,2,1,0:T(8,128)S(1)} %get-tuple-element.1316), kind=kOutput, calls=%fused_computation.102 | convolution fusion | flops 9437190 | bytes 3670040 | tf_op jit(solution)/shard_map/dot_general | solution.py:200
  383.1 7.2 %all-to-all-start.7 = ((f32[16,1,6]{2,1,0:T(1,128)}), f32[16,1,6]{2,1,0:T(1,128)S(1)}, u32[]{:S(2)}, u32[]{:S(2)}) async-start(f32[16,1,6]{2,1,0:T(1,128)} %broadcast_in_dim.36), calls=%async_computation.7 | async-start | bytes 16384 | tf_op jit(solution)/shard_map/all_to_all | solution.py:25
  393.1 4.2 all-to-all-done.7
  461.3 7.5 %fusion.14 = f32[1,8,128,128]{3,0,2,1:T(1,128)S(1)} fusion(f32[6,8,128,128]{3,2,1,0:T(8,128)} %get-tuple-element.1317, f32[6]{0:T(128)S(1)} %constant_dynamic-update-slice_fusion.25), kind=kOutput, calls=%fused_computation.25 | convolution fusion | flops 9437184 | bytes 3670040 | tf_op jit(solution)/shard_map/j,jxyz->xyz/dot_general | solution.py:217
  471.9 12.0 %all_to_all.135 = bf16[2,64,8,128]{3,2,0,1:T(8,128)(2,1)S(1)} all-to-all(bf16[2,64,8,128]{3,2,0,1:T(8,128)(2,1)S(1)} %reshape.3030), channel_id=1, replica_groups=mesh['band'=16,'grid'=16] {'grid'}, dimensions={1} | all-to-all | bytes 524288 | tf_op jit(solution)/shard_map/all_to_all | solution.py:148
  485.0 11.9 %all_to_all.136 = bf16[2,4,128,128]{3,1,0,2:T(4,128)(2,1)S(1)} all-to-all(bf16[2,4,128,128]{3,1,0,2:T(4,128)(2,1)S(1)} %copy.325), channel_id=1, replica_groups=mesh['band'=16,'grid'=16] {'grid'}, dimensions={2} | all-to-all | bytes 524288 | tf_op jit(solution)/shard_map/all_to_all | solution.py:158
  501.7 4.5 fusion.22
  506.3 55.6 %all-gather.11.cloned.1.call-done = bf16[128,128,128]{2,1,0:T(8,128)(2,1)} async-done(((bf16[8,128,128]{2,1,0:T(8,128)(2,1)}), bf16[128,128,128]{2,1,0:T(8,128)(2,1)}) %all-gather.11.cloned.1.call-update) | async-done | bytes 4194320 | tf_op jit(solution)/shard_map/all_gather | solution.py:35
  568.4 9.8 %fusion.77 = f32[6]{0:T(128)S(1)} fusion(f32[8,128,128,1]{2,3,1,0:T(1,128)S(1)} %bitcast.564, f32[6,8,128,128]{3,2,1,0:T(8,128)S(1)} %get-tuple-element.1314), kind=kOutput, calls=%fused_computation.99 | convolution fusion | flops 9437190 | bytes 3670040 | tf_op jit(solution)/shard_map/dot_general | solution.py:198
  578.8 16.8 %all-to-all-start.12 = ((f32[16,1,6]{2,1,0:T(1,128)}), f32[16,1,6]{2,1,0:T(1,128)S(1)}, u32[]{:S(2)}, u32[]{:S(2)}) async-start(f32[16,1,6]{2,1,0:T(1,128)} %broadcast_in_dim.41), calls=%async_computation.12 | async-start | bytes 16384 | tf_op jit(solution)/shard_map/all_to_all | solution.py:25
  595.6 10.8 %fusion.80 = f32[6]{0:T(128)S(1)} fusion(f32[8,128,128,1]{2,3,1,0:T(1,128)} %bitcast.565, f32[6,8,128,128]{3,2,1,0:T(8,128)S(1)} %get-tuple-element.1314), kind=kOutput, calls=%fused_computation.100 | convolution fusion | flops 9437190 | bytes 3670040 | tf_op jit(solution)/shard_map/dot_general | solution.py:200
  607.0 7.2 %all-to-all-start.11 = ((f32[16,1,6]{2,1,0:T(1,128)}), f32[16,1,6]{2,1,0:T(1,128)S(1)}, u32[]{:S(2)}, u32[]{:S(2)}) async-start(f32[16,1,6]{2,1,0:T(1,128)} %broadcast_in_dim.40), calls=%async_computation.11 | async-start | bytes 16384 | tf_op jit(solution)/shard_map/all_to_all | solution.py:25
  616.9 4.3 all-to-all-done.11
  684.6 7.5 %fusion.12 = f32[1,8,128,128]{3,0,2,1:T(1,128)S(1)} fusion(f32[6,8,128,128]{3,2,1,0:T(8,128)} %get-tuple-element.1315, f32[6]{0:T(128)S(1)} %constant_dynamic-update-slice_fusion.24), kind=kOutput, calls=%fused_computation.23 | convolution fusion | flops 9437184 | bytes 3670040 | tf_op jit(solution)/shard_map/j,jxyz->xyz/dot_general | solution.py:217
  (390 shorter events, 119.6 us)
Async XLA Ops:
  12.7 17.3 %all-to-all-start = ((bf16[2,64,8,128]{3,2,0,1:T(8,128)(2,1)}), bf16[2,64,8,128]{3,2,0,1:T(8,128)(2,1)S(1)}, u32[]{:S(2)}, u32[]{:S(2)}) async-start(bf16[2,64,8,128]{3,2,0,1:T(8,128)(2,1)} %reshape.3028), calls=%async_computation | async-start | bytes 524288 | tf_op jit(solution)/shard_map/all_to_all | solution.py:148
  21.1 91.2 %all-gather.7.cloned.1.call-start = ((), (), s32[]{:S(2)}) async-start(), calls=%async_computation.13 | async-start | bytes 4456448 | tf_op jit(solution)/shard_map/all_gather | solution.py:35
  56.7 58.8 %copy-start.16 = (f32[8,128,128]{2,1,0:T(8,128)S(1)}, f32[8,128,128]{2,1,0:T(8,128)}, u32[]{:S(2)}) copy-start(f32[8,128,128]{2,1,0:T(8,128)} %param.227) | copy-start | bytes 1572868
  56.7 58.8 %copy-start.34 = (f32[8,128,128]{2,1,0:T(8,128)S(1)}, f32[8,128,128]{2,1,0:T(8,128)}, u32[]{:S(2)}) copy-start(f32[8,128,128]{2,1,0:T(8,128)} %param.229) | copy-start | bytes 1572868
  56.7 58.8 %copy-start.35 = (f32[8,128,128]{2,1,0:T(8,128)S(1)}, f32[8,128,128]{2,1,0:T(8,128)}, u32[]{:S(2)}) copy-start(f32[8,128,128]{2,1,0:T(8,128)} %param.228) | copy-start | bytes 1572868
  112.3 4.2 copy-start.1
  112.3 4.2 copy-start.6
  129.2 27.9 %all-to-all-start.4 = ((f32[16,1,6]{2,1,0:T(1,128)}), f32[16,1,6]{2,1,0:T(1,128)S(1)}, u32[]{:S(2)}, u32[]{:S(2)}) async-start(f32[16,1,6]{2,1,0:T(1,128)} %broadcast_in_dim.33), calls=%async_computation.4 | async-start | bytes 16384 | tf_op jit(solution)/shard_map/all_to_all | solution.py:25
  157.1 85.8 %copy-start.17 = (f32[8,128,128]{2,1,0:T(8,128)S(1)}, f32[8,128,128]{2,1,0:T(8,128)}, u32[]{:S(2)}) copy-start(f32[8,128,128]{2,1,0:T(8,128)} %param.227) | copy-start | bytes 1572868
  157.1 85.9 %copy-start.20 = (f32[8,128,128]{2,1,0:T(8,128)S(1)}, f32[8,128,128]{2,1,0:T(8,128)}, u32[]{:S(2)}) copy-start(f32[8,128,128]{2,1,0:T(8,128)} %get-tuple-element.1313) | copy-start | bytes 1572868
  157.1 85.9 %copy-start.28 = (f32[8,128,128]{2,1,0:T(8,128)S(1)}, f32[8,128,128]{2,1,0:T(8,128)}, u32[]{:S(2)}) copy-start(f32[8,128,128]{2,1,0:T(8,128)} %param.226) | copy-start | bytes 1572868
  157.7 14.2 %all-to-all-start.2 = ((f32[16,1,6]{2,1,0:T(1,128)}), f32[16,1,6]{2,1,0:T(1,128)S(1)}, u32[]{:S(2)}, u32[]{:S(2)}) async-start(f32[16,1,6]{2,1,0:T(1,128)} %broadcast_in_dim.31), calls=%async_computation.2 | async-start | bytes 16384 | tf_op jit(solution)/shard_map/all_to_all | solution.py:25
  164.9 172.8 %all-gather.9.cloned.1.call-start = ((), (), s32[]{:S(2)}) async-start(), calls=%async_computation.14 | async-start | bytes 4456448 | tf_op jit(solution)/shard_map/all_gather | solution.py:35
  281.4 59.5 %copy-start.21 = (f32[8,128,128]{2,1,0:T(8,128)S(1)}, f32[8,128,128]{2,1,0:T(8,128)}, u32[]{:S(2)}) copy-start(f32[8,128,128]{2,1,0:T(8,128)} %get-tuple-element.1313) | copy-start | bytes 1572868
  281.4 59.5 %copy-start.22 = (f32[8,128,128]{2,1,0:T(8,128)S(1)}, f32[8,128,128]{2,1,0:T(8,128)}, u32[]{:S(2)}) copy-start(f32[8,128,128]{2,1,0:T(8,128)} %get-tuple-element.1311) | copy-start | bytes 1572868
  337.7 4.1 copy-start.3
  337.7 4.1 copy-start.5
  354.6 27.9 %all-to-all-start.8 = ((f32[16,1,6]{2,1,0:T(1,128)}), f32[16,1,6]{2,1,0:T(1,128)S(1)}, u32[]{:S(2)}, u32[]{:S(2)}) async-start(f32[16,1,6]{2,1,0:T(1,128)} %broadcast_in_dim.37), calls=%async_computation.8 | async-start | bytes 16384 | tf_op jit(solution)/shard_map/all_to_all | solution.py:25
  382.4 86.4 %copy-start.18 = (f32[8,128,128]{2,1,0:T(8,128)S(1)}, f32[8,128,128]{2,1,0:T(8,128)}, u32[]{:S(2)}) copy-start(f32[8,128,128]{2,1,0:T(8,128)} %get-tuple-element.1309) | copy-start | bytes 1572868
  382.4 86.4 %copy-start.23 = (f32[8,128,128]{2,1,0:T(8,128)S(1)}, f32[8,128,128]{2,1,0:T(8,128)}, u32[]{:S(2)}) copy-start(f32[8,128,128]{2,1,0:T(8,128)} %get-tuple-element.1311) | copy-start | bytes 1572868
  382.4 86.4 %copy-start.29 = (f32[8,128,128]{2,1,0:T(8,128)S(1)}, f32[8,128,128]{2,1,0:T(8,128)}, u32[]{:S(2)}) copy-start(f32[8,128,128]{2,1,0:T(8,128)} %param.226) | copy-start | bytes 1572868
  383.1 14.2 %all-to-all-start.7 = ((f32[16,1,6]{2,1,0:T(1,128)}), f32[16,1,6]{2,1,0:T(1,128)S(1)}, u32[]{:S(2)}, u32[]{:S(2)}) async-start(f32[16,1,6]{2,1,0:T(1,128)} %broadcast_in_dim.36), calls=%async_computation.7 | async-start | bytes 16384 | tf_op jit(solution)/shard_map/all_to_all | solution.py:25
  390.3 171.6 %all-gather.11.cloned.1.call-start = ((), (), s32[]{:S(2)}) async-start(), calls=%async_computation.15 | async-start | bytes 4456448 | tf_op jit(solution)/shard_map/all_gather | solution.py:35
  506.2 58.9 %copy-start.19 = (f32[8,128,128]{2,1,0:T(8,128)S(1)}, f32[8,128,128]{2,1,0:T(8,128)}, u32[]{:S(2)}) copy-start(f32[8,128,128]{2,1,0:T(8,128)} %get-tuple-element.1309) | copy-start | bytes 1572868
  506.2 58.9 %copy-start.24 = (f32[8,128,128]{2,1,0:T(8,128)S(1)}, f32[8,128,128]{2,1,0:T(8,128)}, u32[]{:S(2)}) copy-start(f32[8,128,128]{2,1,0:T(8,128)} %get-tuple-element.1311) | copy-start | bytes 1572868
  506.2 58.9 %copy-start.30 = (f32[8,128,128]{2,1,0:T(8,128)S(1)}, f32[8,128,128]{2,1,0:T(8,128)}, u32[]{:S(2)}) copy-start(f32[8,128,128]{2,1,0:T(8,128)} %get-tuple-element.1307) | copy-start | bytes 1572868
  561.9 4.1 copy-start.8
  561.9 4.1 copy-start.9
  578.8 27.6 %all-to-all-start.12 = ((f32[16,1,6]{2,1,0:T(1,128)}), f32[16,1,6]{2,1,0:T(1,128)S(1)}, u32[]{:S(2)}, u32[]{:S(2)}) async-start(f32[16,1,6]{2,1,0:T(1,128)} %broadcast_in_dim.41), calls=%async_computation.12 | async-start | bytes 16384 | tf_op jit(solution)/shard_map/all_to_all | solution.py:25
  606.4 85.7 %copy-start.27 = (f32[8,128,128]{2,1,0:T(8,128)S(1)}, f32[8,128,128]{2,1,0:T(8,128)}, u32[]{:S(2)}) copy-start(f32[8,128,128]{2,1,0:T(8,128)} %get-tuple-element.1305) | copy-start | bytes 1572868
  606.4 85.7 %copy-start.31 = (f32[8,128,128]{2,1,0:T(8,128)S(1)}, f32[8,128,128]{2,1,0:T(8,128)}, u32[]{:S(2)}) copy-start(f32[8,128,128]{2,1,0:T(8,128)} %get-tuple-element.1307) | copy-start | bytes 1572868
  607.0 14.2 %all-to-all-start.11 = ((f32[16,1,6]{2,1,0:T(1,128)}), f32[16,1,6]{2,1,0:T(1,128)S(1)}, u32[]{:S(2)}, u32[]{:S(2)}) async-start(f32[16,1,6]{2,1,0:T(1,128)} %broadcast_in_dim.40), calls=%async_computation.11 | async-start | bytes 16384 | tf_op jit(solution)/shard_map/all_to_all | solution.py:25
  (15 other events, 36.3 us)
Sparse Core Ops, SparseCore 0:
  47.3 64.9 all-gather.6
  276.8 60.8 all-gather.8
  501.8 60.0 all-gather.10
where the time goes:
time: 706 us; the launch traced here: 700 us
  waiting for transfers between devices  177 us (25%)
  between operations  150 us (21%)
  matrix products  103 us (15%)
  starting transfers between devices  81.1 us (11%)
  other arithmetic  71.6 us (10%)
  blocking collectives  71.2 us (10%)
  local copies, waits for them, and re-layouts  46.6 us (7%)
    all_gather x3, waiting for transfers between devices, over_pieces(): blocks = lax.all_gather(array, axis).astype(jnp.float32)  156 us
    all_to_all x6, starting transfers between devices, sent_to_all(): lax.all_to_all(jnp.broadcast_to(array[None], (count, *array.shape)), axis...  72.5 us
    all_to_all x3, blocking collectives, local(): lax.all_to_all(spatial.astype(jnp.bfloat16).reshape(item_count, column_ro...  36.2 us
    dot_general x3, matrix products, local(): jnp.dot(flat_diffs, mixing_residual.reshape(-1), precision=highest)  32.4 us
    dot_general x3, matrix products, local(): jnp.dot(flat_diffs, newest.reshape(-1), precision=highest) / cells_total  29.3 us
    all_to_all x2, blocking collectives, local(): lax.all_to_all(along_y, 'grid', split_axis=1, concat_axis=2, tiled=True)  24 us
    dot_general x3, matrix products, local(): jnp.einsum('j,jxyz->xyz', coeffs, combined, precision=highest)  22.4 us
  transfers between devices with their start and end apart: 10, of which 7 were waited for; matrix products, arithmetic and copies ran while one was open for 8% of the time, Pallas kernels for 0%

commit v1 on v0

v1 whole, which is shorter than its diff:
```python
import math

import jax
import jax.numpy as jnp
import ml_dtypes
import numpy as np
from jax import lax
from jax.experimental import pallas as pl
from jax.experimental.pallas import tpu as pltpu
from jax.sharding import PartitionSpec as P

NG = 128
KEPT = NG // 2
DEPTH = 6
ITERS = 3
F32 = jnp.float32
BF16 = jnp.bfloat16
MESH = pl.DeviceIdType.MESH

time_step = 0.25
energy_shift = 2.5
mixing_weight = 0.5
ridge_share = 0.1
ridge_floor = 0.01
density_scale = 8.0
bands_total = 32


def tables():
    frequency = np.arange(-(NG // 4), NG // 4, dtype=np.int32)
    positions = np.arange(NG, dtype=np.int32)
    phase = (positions[:, None] * frequency[None, :]) % NG
    angles = phase.astype(np.float32) * np.float32(2.0 * math.pi / NG)
    unit = np.float32(1.0 / math.sqrt(NG))
    cosine = (np.cos(angles) * unit).astype(ml_dtypes.bfloat16)
    sine = (np.sin(angles) * unit).astype(ml_dtypes.bfloat16)
    forward_z = np.concatenate(
        [np.concatenate([cosine, -sine], 1), np.concatenate([sine, cosine], 1)], 0
    )
    inverse_z = np.concatenate(
        [np.concatenate([cosine.T, sine.T], 1), np.concatenate([-sine.T, cosine.T], 1)], 0
    )
    stacked = np.concatenate([cosine.T, sine.T], 0)
    beside = np.concatenate([cosine, sine], 1)
    return forward_z, inverse_z, stacked, beside


def dot(a, b):
    return jnp.dot(a, b, preferred_element_type=F32)


def kernel(
    occ, bands, ext, den, pden, pres, hden, hres, wzf, wzi, fcs, ics,
    out_d, out_r,
    bands_v, ext_v, den_v, facg, facp, plane, rs, qs, psi,
    send_f, recv_f, stage, kin, send_b, recv_b, part, recv_d, row_s, rows, occ_s, occs,
    outs_s, outs_v,
    in_sems, pl_sems, pl_send, sf_sem, rf_sem, sb_sem, rb_sems, sd_sem, rd_sems,
    sr_sem, rr_sem, so_sem, ro_sem, sout_sems, rout_sems,
):
    g = lax.axis_index("band")
    i = lax.axis_index("grid")
    core = i % 2
    xy = i // 2
    half = g // 8
    zz = g % 8
    me = xy * 16 + g
    twin = i + 1 - 2 * core

    def remote(src, dst, ssem, rsem, dg, di):
        return pltpu.make_async_remote_copy(
            src_ref=src, dst_ref=dst, send_sem=ssem, recv_sem=rsem,
            device_id=(dg, di), device_id_type=MESH,
        )

    def drain(ref, sem):
        pltpu.make_async_copy(ref, ref, sem).wait()

    loads = [
        pltpu.make_async_copy(ext, ext_v, in_sems.at[0]),
        pltpu.make_async_copy(den, den_v, in_sems.at[1]),
        pltpu.make_async_copy(bands, bands_v, in_sems.at[2]),
    ]
    for load in loads:
        load.start()

    owner = core == half

    @pl.when(owner)
    def _():
        pieces = [
            (ext.at[zz], plane.at[0], 0), (den.at[zz], plane.at[1], 0),
            (pden.at[zz], plane.at[2], 0), (pres.at[zz], plane.at[3], 0),
            (hden.at[:, zz], rs.at[pl.ds(0, DEPTH - 1)], 1),
            (hres.at[:, zz], qs.at[pl.ds(0, DEPTH - 1)], 2),
        ]
        for src, dst, s in pieces:
            pltpu.make_async_copy(src, dst, pl_sems.at[s]).start()
            remote(src, dst, pl_send.at[s], pl_sems.at[s], g, twin).start()

    occ_row = jnp.full((1, NG), occ[core], F32)
    occ_s[...] = occ_row
    occs[g] = occ_row

    def send_occ(n, c):
        remote(occ_s, occs.at[g], so_sem, ro_sem, (g + n) % 16, i).start()
        return c

    lax.fori_loop(1, 16, send_occ, 0)

    lane = lax.broadcasted_iota(jnp.int32, (KEPT, NG), 1)
    sgn_f = jnp.where(lane < KEPT, 1.0, -1.0).astype(F32)
    sgn_i = -sgn_f
    fz = (lane % KEPT - NG // 4).astype(F32)
    fx = (lax.broadcasted_iota(jnp.int32, (KEPT, NG), 0) - NG // 4).astype(F32)
    quarter = NG / 4.0
    for r in range(8):
        fy = (8 * xy + r - NG // 4).astype(F32)
        kin[r] = jnp.exp((fx * fx + fy * fy + fz * fz) * (-time_step / (quarter * quarter)))

    def forward_zy(w):
        a = dot(w, wzf[...]).astype(BF16)
        pq = dot(fcs[...], a)
        b = pq[:KEPT] + pltpu.roll(pq[KEPT:], KEPT, 1) * sgn_f
        return b.reshape(8, 8, NG).astype(BF16)

    def send_tile(src, dst, ssem, rsem, dg, di, same):
        @pl.when(same)
        def _():
            pltpu.make_async_copy(src, dst, rsem).start()

        @pl.when(jnp.logical_not(same))
        def _():
            remote(src, dst, ssem, rsem, dg, di).start()

    def spectral():
        drain(recv_f, rf_sem)
        stage[...] = recv_f[...].astype(F32).reshape(8 * NG, NG)
        for r in range(8):
            x = stage[pl.ds(r, NG, stride=8), :].astype(BF16)
            pq = dot(fcs[...], x)
            c = (pq[:KEPT] + pltpu.roll(pq[KEPT:], KEPT, 1) * sgn_f) * kin[r]
            c2 = pltpu.roll(c, KEPT, 1) * sgn_i
            both = jnp.concatenate([c, c2], axis=0).astype(BF16)
            stage[pl.ds(r, NG, stride=8), :] = dot(ics[...], both)
        send_b[...] = stage[...].reshape(NG, 8, NG).astype(BF16)

        def send(n, carry):
            p = (me + n) % 128
            send_tile(
                send_b.at[p], recv_b.at[g * 8 + xy], sb_sem, rb_sems.at[g],
                p % 16, 2 * (p // 16) + core, n == 0,
            )
            return carry

        lax.fori_loop(0, 128, send, 0)

    def backward(n, carry):
        t = (g + n) % 16
        tiles = recv_b.at[pl.ds(t * 8, 8)]
        drain(tiles, rb_sems.at[t])
        d = tiles[...].astype(F32).reshape(KEPT, NG)
        d2 = pltpu.roll(d, KEPT, 1) * sgn_i
        both = jnp.concatenate([d, d2], axis=0).astype(BF16)
        e = dot(ics[...], both).astype(BF16)
        new = dot(e, wzi[...]).astype(BF16)
        psi[t] = new
        wide = new.astype(F32)
        re, im = wide[:, :NG], wide[:, NG:]
        part[...] += occs[t] * (re * re + im * im)
        return carry

    gram = None
    for step in range(ITERS):
        if step == 0:
            for load in loads:
                load.wait()
            facg[...] = jnp.exp(-time_step * (ext_v[...] + den_v[...] - energy_shift))

            def forward(n, carry):
                which, j = n // 8, n % 8
                f = facg[j]
                w = jnp.concatenate(
                    [bands_v[0, which, j].astype(F32) * f, bands_v[1, which, j].astype(F32) * f],
                    axis=1,
                ).astype(BF16)
                send_f[pl.ds(n * 8, 8)] = forward_zy(w)
                for m in range(8):
                    q = (xy + m) % 8
                    di = 2 * q + which
                    send_tile(
                        send_f.at[n * 8 + q], recv_f.at[8 * i + j], sf_sem, rf_sem, g, di, di == i
                    )
                return carry

            lax.fori_loop(0, 16, forward, 0)
            drain(send_f.at[pl.ds(0, 120)], sf_sem)
        else:
            def forward(n, carry):
                t = (g + n) % 16
                f = facp[...]
                w = (psi[t].astype(F32) * jnp.concatenate([f, f], axis=1)).astype(BF16)
                send_f[pl.ds(t * 8, 8)] = forward_zy(w)
                for m in range(8):
                    q = (xy + m) % 8
                    send_tile(
                        send_f.at[t * 8 + q], recv_f.at[me], sf_sem, rf_sem,
                        t, 2 * q + core, jnp.logical_and(n == 0, m == 0),
                    )
                return carry

            lax.fori_loop(0, 16, forward, 0)
            drain(send_f.at[pl.ds(0, 127)], sf_sem)

        spectral()

        if step == 0:
            drain(plane, pl_sems.at[0])
            drain(rs.at[pl.ds(0, DEPTH - 1)], pl_sems.at[1])
            drain(qs.at[pl.ds(0, DEPTH - 1)], pl_sems.at[2])
            drain(occs.at[pl.ds(0, 15)], ro_sem)
            drain(occs.at[pl.ds(0, 15)], so_sem)

            @pl.when(owner)
            def _():
                drain(plane, pl_send.at[0])
                drain(rs.at[pl.ds(0, DEPTH - 1)], pl_send.at[1])
                drain(qs.at[pl.ds(0, DEPTH - 1)], pl_send.at[2])

        part[...] = jnp.zeros_like(part)
        lax.fori_loop(0, 16, backward, 0)
        drain(send_b.at[pl.ds(0, 127)], sb_sem)

        swap = remote(part, recv_d.at[step], sd_sem, rd_sems.at[step], g, twin)
        swap.start()
        swap.wait()
        rho_out = (part[...] + recv_d[step]) * (density_scale / bands_total)
        rho_in = plane[1]
        res = rho_out - rho_in
        newest = res - plane[3]
        rs[DEPTH - 1 + step] = rho_in - plane[2]
        qs[DEPTH - 1 + step] = newest

        def rows_of(a):
            return a.reshape(16, 8, NG)

        lanes = lax.broadcasted_iota(jnp.int32, (1, NG), 1)
        row = jnp.zeros((1, NG), F32)

        def put(row, at, a, b):
            total = jnp.sum(jnp.sum(rows_of(a * b), axis=0), axis=0, keepdims=True)
            return jnp.where(lanes == at, jnp.sum(total, axis=1, keepdims=True), row)

        for j in range(DEPTH):
            q = qs[step + j]
            row = put(row, j, q, newest)
            row = put(row, DEPTH + j, q, res)
        if step == 0:
            at = 2 * DEPTH
            for a in range(DEPTH - 1):
                for b in range(a + 1):
                    row = put(row, at, qs[a], qs[b])
                    at += 1
        row_s[...] = row
        rows[me] = row

        def send_row(n, carry):
            p = (me + n) % 128
            remote(row_s, rows.at[me], sr_sem, rr_sem, p % 16, 2 * (p // 16) + core).start()
            return carry

        lax.fori_loop(1, 128, send_row, 0)

        def gather(value, which):
            outs_s[which] = value.astype(BF16)

            def send(n, carry):
                dg = (g + n) % 16
                di = 2 * xy + half
                same = jnp.logical_and(n == 0, di == i)
                send_tile(
                    outs_s.at[which, pl.ds(pl.multiple_of(core * KEPT, KEPT), KEPT)],
                    outs_v.at[which, 2 * zz + core],
                    sout_sems.at[which], rout_sems.at[which], dg, di, same,
                )
                return carry

            lax.fori_loop(0, 16, send, 0)

        if step == ITERS - 1:
            gather(res, 1)

        drain(rows.at[pl.ds(0, 127)], rr_sem)
        drain(rows.at[pl.ds(0, 127)], sr_sem)
        sums = jnp.sum(rows[...], axis=0) * (1.0 / (NG * NG * NG))

        def splat(at):
            return jnp.broadcast_to(sums[:, at : at + 1], (8, NG))

        border = [splat(j) for j in range(DEPTH)]
        right = [splat(DEPTH + j) for j in range(DEPTH)]
        if step == 0:
            at = 2 * DEPTH
            gram = []
            for a in range(DEPTH - 1):
                gram.append([splat(at + b) for b in range(a + 1)])
                at += a + 1
        else:
            gram = [[gram[a][b] for b in range(1, a + 1)] for a in range(1, DEPTH)]
        gram.append(border)
        trace = gram[0][0]
        for j in range(1, DEPTH):
            trace = trace + gram[j][j]
        ridge = trace * (ridge_share / DEPTH) + ridge_floor
        low = [[None] * DEPTH for _ in range(DEPTH)]
        scaled = [[None] * DEPTH for _ in range(DEPTH)]
        inverse = [None] * DEPTH
        for c in range(DEPTH):
            value = gram[c][c] + ridge
            for k in range(c):
                value = value - scaled[c][k] * low[c][k]
            inverse[c] = 1.0 / value
            for r in range(c + 1, DEPTH):
                value = gram[r][c]
                for k in range(c):
                    value = value - scaled[r][k] * low[c][k]
                scaled[r][c] = value
                low[r][c] = value * inverse[c]
        middle = []
        for r in range(DEPTH):
            value = right[r]
            for k in range(r):
                value = value - low[r][k] * middle[k]
            middle.append(value)
        coeffs = [None] * DEPTH
        for r in reversed(range(DEPTH)):
            value = middle[r] * inverse[r]
            for k in range(r + 1, DEPTH):
                value = value - low[k][r] * coeffs[k]
            coeffs[r] = value
        mixed = rows_of(rho_in + mixing_weight * res)
        for j in range(DEPTH):
            mixed = mixed - coeffs[j][None] * rows_of(rs[step + j] + mixing_weight * qs[step + j])
        rho = mixed.reshape(NG, NG)
        if step < ITERS - 1:
            plane[2] = rho_in
            plane[3] = res
            plane[1] = rho
            facp[...] = jnp.exp(-time_step * (plane[0] + rho - energy_shift))
        else:
            gather(rho, 0)
            for which, out in ((1, out_r), (0, out_d)):
                drain(outs_v.at[which], rout_sems.at[which])
                out[...] = outs_v[which].astype(F32).reshape(8, NG, NG)

                @pl.when(owner)
                def _():
                    drain(outs_v.at[which, pl.ds(0, 15)], sout_sems.at[which])

                @pl.when(jnp.logical_not(owner))
                def _():
                    drain(outs_v.at[which], sout_sems.at[which])


def local(bands, occupations, external, density_in, prev_density, prev_residual, hist_density, hist_residual):
    constants = [jnp.asarray(t) for t in tables()]
    slab = external.shape
    hbm = pl.BlockSpec(memory_space=pl.ANY)
    vmem = pl.BlockSpec(memory_space=pltpu.VMEM)
    smem = pl.BlockSpec(memory_space=pltpu.SMEM)
    dma = pltpu.SemaphoreType.DMA
    out = jax.ShapeDtypeStruct(slab, F32)
    return pl.pallas_call(
        kernel,
        out_shape=(out, out),
        in_specs=[smem] + [hbm] * 7 + [vmem] * 4,
        out_specs=(vmem, vmem),
        scratch_shapes=[
            pltpu.VMEM(bands.shape, BF16),
            pltpu.VMEM(slab, F32),
            pltpu.VMEM(slab, F32),
            pltpu.VMEM(slab, F32),
            pltpu.VMEM((NG, NG), F32),
            pltpu.VMEM((4, NG, NG), F32),
            pltpu.VMEM((DEPTH - 1 + ITERS, NG, NG), F32),
            pltpu.VMEM((DEPTH - 1 + ITERS, NG, NG), F32),
            pltpu.VMEM((16, NG, 2 * NG), BF16),
            pltpu.VMEM((128, 8, NG), BF16),
            pltpu.VMEM((128, 8, NG), BF16),
            pltpu.VMEM((8 * NG, NG), F32),
            pltpu.VMEM((8, KEPT, NG), F32),
            pltpu.VMEM((128, 8, NG), BF16),
            pltpu.VMEM((128, 8, NG), BF16),
            pltpu.VMEM((NG, NG), F32),
            pltpu.VMEM((ITERS, NG, NG), F32),
            pltpu.VMEM((1, NG), F32),
            pltpu.VMEM((128, 1, NG), F32),
            pltpu.VMEM((1, NG), F32),
            pltpu.VMEM((16, 1, NG), F32),
            pltpu.VMEM((2, NG, NG), BF16),
            pltpu.VMEM((2, 16, KEPT, NG), BF16),
            dma((3,)), dma((3,)), dma((3,)),
            dma(()), dma(()), dma(()), dma((16,)), dma(()), dma((ITERS,)),
            dma(()), dma(()), dma(()), dma(()), dma((2,)), dma((2,)),
        ],
        compiler_params=pltpu.CompilerParams(
            has_side_effects=True, vmem_limit_bytes=48 * 1024 * 1024
        ),
        name="scf",
    )(
        occupations, bands, external, density_in, prev_density, prev_residual,
        hist_density, hist_residual, *constants,
    )


def solution(mesh):
    placed = (
        P(None, "band", "grid", None, None),
        P("band"),
        P("grid", None, None),
        P("grid", None, None),
        P("grid", None, None),
        P("grid", None, None),
        P(None, "grid", None, None),
        P(None, "grid", None, None),
    )
    return jax.shard_map(
        local,
        mesh=mesh,
        in_specs=placed,
        out_specs=(P("grid", None, None), P("grid", None, None)),
        check_vma=False,
    )
```

time: 706 us -> 152 us (0.22)
  waiting for transfers between devices: 177 us -> 0 us
  between operations: 150 us -> 0.66 us
  Pallas kernels: 0 us -> 140 us
  matrix products: 103 us -> 0 us
  starting transfers between devices: 81.1 us -> 0 us
  other arithmetic: 71.6 us -> 0 us
  blocking collectives: 71.2 us -> 0 us
  local copies, waits for them, and re-layouts: 46.6 us -> 10.8 us
    all_gather x3 -> x0, waiting for transfers between devices: 156 us -> none  [over_pieces(): blocks = lax.all_gather(array, axis).astype(jnp.float32)]
    pallas_call x0 -> x1, Pallas kernels: none -> 140 us  [local(): pl.pallas_call(kernel, out_shape=(out, out), in_specs=[smem] + [hbm] * 7...]
    dot_general x25 -> x0, matrix products: 103 us -> none  [the longest x3 32.4 us: local(): jnp.dot(flat_diffs, mixing_residual.reshape(-1), precision=highest)]
    all_to_all x7 -> x0, starting transfers between devices: 80.9 us -> none  [the longest x6 72.5 us: sent_to_all(): lax.all_to_all(jnp.broadcast_to(array[None], (count, *array.shape)), axis...]
    all_to_all x6 -> x0, blocking collectives: 71.2 us -> none  [the longest x3 36.2 us: local(): lax.all_to_all(spatial.astype(jnp.bfloat16).reshape(item_count, column_ro...]
    reduce_sum x67 -> x0, other arithmetic: 44.8 us -> none  [the longest x18 11.3 us: solve_definite(): jnp.sum(factor_low[row_index, :column] * factor_low[column, :column])]
    all_to_all x7 -> x0, waiting for transfers between devices: 20.8 us -> none  [the longest x6 12.8 us: sent_to_all(): lax.all_to_all(jnp.broadcast_to(array[None], (count, *array.shape)), axis...]
    slice x44 -> x0, local copies, waits for them, and re-layouts: 20.5 us -> none  [the longest x12 7.13 us: solve_definite(): factor_low[column, :column]]
  transfers between devices with their start and end apart: 10 -> 0, of which waited for: 7 -> 0; matrix products, arithmetic and copies ran while one was open for 8% -> 0% of each run, Pallas kernels for 0% -> 0%
where the time goes in v1:
time: 152 us; the launch traced here: 151 us
  Pallas kernels  140 us (92%)
  local copies, waits for them, and re-layouts  10.8 us (7%)
    pallas_call x1, Pallas kernels, local(): pl.pallas_call(kernel, out_shape=(out, out), in_specs=[smem] + [hbm] * 7...  140 us
    unnamed x22, local copies, waits for them, and re-layouts  10.8 us

profile of v1, /device:TPU:1, one launch (start us, length us, event | category | flops | bytes accessed | tf_op | source)
XLA Modules:
  0.0 151.2 jit_solution(15626940194132659133)
XLA Ops:
  0.6 0.0 copy-start
  0.6 1.2 copy-done
  1.9 0.0 copy-start.1
  1.9 1.0 copy-done.1
  2.9 0.0 copy-start.2
  2.9 1.0 copy-done.2
  3.9 0.0 copy-start.3
  3.9 1.0 copy-done.3
  5.0 0.0 copy-start.4
  5.0 1.0 copy-done.4
  6.0 0.0 copy-start.5
  6.0 0.8 copy-done.5
  6.9 0.0 copy-start.6
  6.9 0.8 copy-done.6
  7.7 0.0 copy-start.7
  7.7 0.8 copy-done.7
  8.5 0.0 copy-start.8
  8.5 0.8 copy-done.8
  9.2 0.0 copy-start.9
  9.2 0.7 copy-done.9
  9.9 139.7 %scf.1 = (f32[8,128,128]{2,1,0:T(8,128)S(1)}, f32[8,128,128]{2,1,0:T(8,128)S(1)}) custom-call(f32[2]{0:T(128)S(1)} %copy-done.9, bf16[2,2,8,128,128]{4,3,2,1,0:T(8,128)(2,1)S(1)} %copy-done, f32[8,128,128]{2,1,0:T(8,128)S(1)} %copy-done.1, f32[8,128,128]{2,1,0:T(8,128)S(1)} %copy-done.2, f32[8,128,128]{2,1,0:T(8,128)S(1)} %copy-done.3, ...), custom_call_target="tpu_custom_call" | custom-call | tf_op jit(solution)/shard_map/scf/pallas_call | solution.py:373
  149.6 0.8 copy.16
  150.4 0.8 copy.17
Async XLA Ops:
  0.6 1.2 copy-start
  1.9 1.0 copy-start.1
  2.9 1.0 copy-start.2
  3.9 1.0 copy-start.3
  5.0 1.0 copy-start.4
  6.0 0.8 copy-start.5
  6.9 0.8 copy-start.6
  7.7 0.8 copy-start.7
  8.5 0.8 copy-start.8
  9.2 0.7 copy-start.9

commit v2 on v1

--- a/solution.py
+++ b/solution.py
@@ -42,7 +42,9 @@
     )
     stacked = np.concatenate([cosine.T, sine.T], 0)
     beside = np.concatenate([cosine, sine], 1)
-    return forward_z, inverse_z, stacked, beside
+    return np.concatenate(
+        [forward_z, stacked, beside, inverse_z[:, :NG], inverse_z[:, NG:]], 0
+    )
 
 
 def dot(a, b):
@@ -50,9 +52,9 @@
 
 
 def kernel(
-    occ, bands, ext, den, pden, pres, hden, hres, wzf, wzi, fcs, ics,
+    occ, bands, ext, den, pden, pres, hden, hres, mats,
     out_d, out_r,
-    bands_v, ext_v, den_v, facg, facp, plane, rs, qs, psi,
+    mats_v, bands_v, ext_v, den_v, facg, facp, plane, rs, qs, psi,
     send_f, recv_f, stage, kin, send_b, recv_b, part, recv_d, row_s, rows, occ_s, occs,
     outs_s, outs_v,
     in_sems, pl_sems, pl_send, sf_sem, rf_sem, sb_sem, rb_sems, sd_sem, rd_sems,
@@ -80,6 +82,7 @@
         pltpu.make_async_copy(ext, ext_v, in_sems.at[0]),
         pltpu.make_async_copy(den, den_v, in_sems.at[1]),
         pltpu.make_async_copy(bands, bands_v, in_sems.at[2]),
+        pltpu.make_async_copy(mats, mats_v, in_sems.at[3]),
     ]
     for load in loads:
         load.start()
@@ -118,13 +121,40 @@
         fy = (8 * xy + r - NG // 4).astype(F32)
         kin[r] = jnp.exp((fx * fx + fy * fy + fz * fz) * (-time_step / (quarter * quarter)))
 
+    def z_of(m):
+        return (zz + 4 + (1 - 2 * (m % 2)) * ((m + 1) // 2)) % 8
+
+    cols = [
+        ((xy // 2 + dx) % 4) * 2 + (xy + dy) % 2 for dx in (2, 1, 3, 0) for dy in (1, 0)
+    ]
+    halves = [1 - half, half]
+
+    wzf, fcs, ics = mats_v.at[pl.ds(0, 2 * NG)], mats_v.at[pl.ds(2 * NG, NG)], mats_v.at[pl.ds(3 * NG, NG)]
+    wzi = mats_v.at[pl.ds(4 * NG, NG)], mats_v.at[pl.ds(5 * NG, NG)]
+
+    def turned(a):
+        return pltpu.roll(a, KEPT, 1)
+
+    def pair_forward(x):
+        pq = dot(fcs[...], x)
+        return [
+            pq[:KEPT, c : c + NG] + turned(pq[KEPT:, c : c + NG]) * sgn_f for c in (0, NG)
+        ]
+
+    def pair_inverse(d):
+        both = [jnp.concatenate([v, turned(v) * sgn_i], axis=0).astype(BF16) for v in d]
+        return dot(ics[...], jnp.concatenate(both, axis=1))
+
     def forward_zy(w):
         a = dot(w, wzf[...]).astype(BF16)
-        pq = dot(fcs[...], a)
-        b = pq[:KEPT] + pltpu.roll(pq[KEPT:], KEPT, 1) * sgn_f
-        return b.reshape(8, 8, NG).astype(BF16)
-
-    def send_tile(src, dst, ssem, rsem, dg, di, same):
+        b = pair_forward(jnp.concatenate([a[:NG], a[NG:]], axis=1))
+        return [v.reshape(8, 8, NG).astype(BF16) for v in b]
+
+    def send_tile(src, dst, ssem, rsem, dg, di, same=None):
+        if same is None:
+            remote(src, dst, ssem, rsem, dg, di).start()
+            return
+
         @pl.when(same)
         def _():
             pltpu.make_async_copy(src, dst, rsem).start()
@@ -136,38 +166,47 @@
     def spectral():
         drain(recv_f, rf_sem)
         stage[...] = recv_f[...].astype(F32).reshape(8 * NG, NG)
-        for r in range(8):
-            x = stage[pl.ds(r, NG, stride=8), :].astype(BF16)
-            pq = dot(fcs[...], x)
-            c = (pq[:KEPT] + pltpu.roll(pq[KEPT:], KEPT, 1) * sgn_f) * kin[r]
-            c2 = pltpu.roll(c, KEPT, 1) * sgn_i
-            both = jnp.concatenate([c, c2], axis=0).astype(BF16)
-            stage[pl.ds(r, NG, stride=8), :] = dot(ics[...], both)
+        for r in range(0, 8, 2):
+            x = [stage[pl.ds(r + c, NG, stride=8), :].astype(BF16) for c in range(2)]
+            b = pair_forward(jnp.concatenate(x, axis=1))
+            y = pair_inverse([b[c] * kin[r + c] for c in range(2)])
+            for c in range(2):
+                stage[pl.ds(r + c, NG, stride=8), :] = y[:, c * NG : (c + 1) * NG]
         send_b[...] = stage[...].reshape(NG, 8, NG).astype(BF16)
 
-        def send(n, carry):
-            p = (me + n) % 128
-            send_tile(
-                send_b.at[p], recv_b.at[g * 8 + xy], sb_sem, rb_sems.at[g],
-                p % 16, 2 * (p // 16) + core, n == 0,
-            )
+        def send(m, carry):
+            z = z_of(m)
+            for h in range(2):
+                dg = halves[h] * 8 + z
+                for n, q in enumerate(cols):
+                    send_tile(
+                        send_b.at[q * 16 + dg], recv_b.at[g * 8 + xy], sb_sem, rb_sems.at[g],
+                        dg, 2 * q + core, m == 7 if h == 1 and n == 7 else None,
+                    )
             return carry
 
-        lax.fori_loop(0, 128, send, 0)
-
-    def backward(n, carry):
-        t = (g + n) % 16
-        tiles = recv_b.at[pl.ds(t * 8, 8)]
-        drain(tiles, rb_sems.at[t])
-        d = tiles[...].astype(F32).reshape(KEPT, NG)
-        d2 = pltpu.roll(d, KEPT, 1) * sgn_i
-        both = jnp.concatenate([d, d2], axis=0).astype(BF16)
-        e = dot(ics[...], both).astype(BF16)
-        new = dot(e, wzi[...]).astype(BF16)
-        psi[t] = new
-        wide = new.astype(F32)
-        re, im = wide[:, :NG], wide[:, NG:]
-        part[...] += occs[t] * (re * re + im * im)
+        lax.fori_loop(0, 8, send, 0)
+
+    def backward(m, carry):
+        z = z_of(m)
+        ts = [halves[h] * 8 + z for h in range(2)]
+        d = []
+        for t in ts:
+            tiles = recv_b.at[pl.ds(t * 8, 8)]
+            drain(tiles, rb_sems.at[t])
+            d.append(tiles[...].astype(F32).reshape(KEPT, NG))
+        e = pair_inverse(d)
+        e = jnp.concatenate([e[:, :NG], e[:, NG:]], axis=0).astype(BF16)
+        re = dot(e, wzi[0][...]).astype(BF16)
+        im = dot(e, wzi[1][...]).astype(BF16)
+        total = part[...]
+        for h, t in enumerate(ts):
+            mine = slice(h * NG, (h + 1) * NG)
+            psi[t, :, :NG] = re[mine]
+            psi[t, :, NG:] = im[mine]
+            wide_re, wide_im = re[mine].astype(F32), im[mine].astype(F32)
+            total = total + occs[t] * (wide_re * wide_re + wide_im * wide_im)
+        part[...] = total
         return carry
 
     gram = None
@@ -177,39 +216,49 @@
                 load.wait()
             facg[...] = jnp.exp(-time_step * (ext_v[...] + den_v[...] - energy_shift))
 
-            def forward(n, carry):
-                which, j = n // 8, n % 8
-                f = facg[j]
-                w = jnp.concatenate(
-                    [bands_v[0, which, j].astype(F32) * f, bands_v[1, which, j].astype(F32) * f],
-                    axis=1,
-                ).astype(BF16)
-                send_f[pl.ds(n * 8, 8)] = forward_zy(w)
-                for m in range(8):
-                    q = (xy + m) % 8
-                    di = 2 * q + which
-                    send_tile(
-                        send_f.at[n * 8 + q], recv_f.at[8 * i + j], sf_sem, rf_sem, g, di, di == i
-                    )
-                return carry
-
-            lax.fori_loop(0, 16, forward, 0)
+            def make_forward(which, own):
+                def forward(n, carry):
+                    w = []
+                    for c in range(2):
+                        f = facg[2 * n + c]
+                        w.append(jnp.concatenate(
+                            [bands_v[p, which, 2 * n + c].astype(F32) * f for p in range(2)], axis=1
+                        ).astype(BF16))
+                    b = forward_zy(jnp.concatenate(w, axis=0))
+                    for c in range(2):
+                        at = own * 64 + (2 * n + c) * 8
+                        send_f[pl.ds(at, 8)] = b[c]
+                        for k, q in enumerate(cols):
+                            src, dst = send_f.at[at + q], recv_f.at[8 * i + 2 * n + c]
+                            if own and k == 7:
+                                pltpu.make_async_copy(src, dst, rf_sem).start()
+                            else:
+                                send_tile(src, dst, sf_sem, rf_sem, g, 2 * q + which)
+                    return carry
+
+                return forward
+
+            lax.fori_loop(0, 4, make_forward(1 - core, 0), 0)
+            lax.fori_loop(0, 4, make_forward(core, 1), 0)
             drain(send_f.at[pl.ds(0, 120)], sf_sem)
         else:
-            def forward(n, carry):
-                t = (g + n) % 16
+            def forward(m, carry):
+                z = z_of(m)
                 f = facp[...]
-                w = (psi[t].astype(F32) * jnp.concatenate([f, f], axis=1)).astype(BF16)
-                send_f[pl.ds(t * 8, 8)] = forward_zy(w)
-                for m in range(8):
-                    q = (xy + m) % 8
-                    send_tile(
-                        send_f.at[t * 8 + q], recv_f.at[me], sf_sem, rf_sem,
-                        t, 2 * q + core, jnp.logical_and(n == 0, m == 0),
-                    )
+                f = jnp.concatenate([f, f], axis=1)
+                ts = [halves[h] * 8 + z for h in range(2)]
+                w = jnp.concatenate([(psi[t].astype(F32) * f).astype(BF16) for t in ts], axis=0)
+                b = forward_zy(w)
+                for h, t in enumerate(ts):
+                    send_f[pl.ds(t * 8, 8)] = b[h]
+                    for n, q in enumerate(cols):
+                        send_tile(
+                            send_f.at[t * 8 + q], recv_f.at[me], sf_sem, rf_sem,
+                            t, 2 * q + core, m == 7 if h == 1 and n == 7 else None,
+                        )
                 return carry
 
-            lax.fori_loop(0, 16, forward, 0)
+            lax.fori_loop(0, 8, forward, 0)
             drain(send_f.at[pl.ds(0, 127)], sf_sem)
 
         spectral()
@@ -228,7 +277,7 @@
                 drain(qs.at[pl.ds(0, DEPTH - 1)], pl_send.at[2])
 
         part[...] = jnp.zeros_like(part)
-        lax.fori_loop(0, 16, backward, 0)
+        lax.fori_loop(0, 8, backward, 0)
         drain(send_b.at[pl.ds(0, 127)], sb_sem)
 
         swap = remote(part, recv_d.at[step], sd_sem, rd_sems.at[step], g, twin)
@@ -264,28 +313,36 @@
         row_s[...] = row
         rows[me] = row
 
-        def send_row(n, carry):
-            p = (me + n) % 128
-            remote(row_s, rows.at[me], sr_sem, rr_sem, p % 16, 2 * (p // 16) + core).start()
+        def send_row(m, carry):
+            z = z_of(m)
+            for h in range(2):
+                for n, q in enumerate(cols):
+                    copy = remote(
+                        row_s, rows.at[me], sr_sem, rr_sem, halves[h] * 8 + z, 2 * q + core
+                    )
+                    if h == 1 and n == 7:
+                        pl.when(m != 7)(copy.start)
+                    else:
+                        copy.start()
             return carry
 
-        lax.fori_loop(1, 128, send_row, 0)
+        lax.fori_loop(0, 8, send_row, 0)
 
         def gather(value, which):
             outs_s[which] = value.astype(BF16)
 
-            def send(n, carry):
-                dg = (g + n) % 16
-                di = 2 * xy + half
-                same = jnp.logical_and(n == 0, di == i)
-                send_tile(
-                    outs_s.at[which, pl.ds(pl.multiple_of(core * KEPT, KEPT), KEPT)],
-                    outs_v.at[which, 2 * zz + core],
-                    sout_sems.at[which], rout_sems.at[which], dg, di, same,
-                )
+            def send(m, carry):
+                z = z_of(m)
+                for h in range(2):
+                    send_tile(
+                        outs_s.at[which, pl.ds(pl.multiple_of(core * KEPT, KEPT), KEPT)],
+                        outs_v.at[which, 2 * zz + core], sout_sems.at[which], rout_sems.at[which],
+                        halves[h] * 8 + z, 2 * xy + half,
+                        jnp.logical_and(m == 7, owner) if h == 1 else None,
+                    )
                 return carry
 
-            lax.fori_loop(0, 16, send, 0)
+            lax.fori_loop(0, 8, send, 0)
 
         if step == ITERS - 1:
             gather(res, 1)
@@ -363,9 +420,8 @@
 
 
 def local(bands, occupations, external, density_in, prev_density, prev_residual, hist_density, hist_residual):
-    constants = [jnp.asarray(t) for t in tables()]
     slab = external.shape
-    hbm = pl.BlockSpec(memory_space=pl.ANY)
+    hbm = pl.BlockSpec(memory_space=pltpu.HBM)
     vmem = pl.BlockSpec(memory_space=pltpu.VMEM)
     smem = pl.BlockSpec(memory_space=pltpu.SMEM)
     dma = pltpu.SemaphoreType.DMA
@@ -373,9 +429,10 @@
     return pl.pallas_call(
         kernel,
         out_shape=(out, out),
-        in_specs=[smem] + [hbm] * 7 + [vmem] * 4,
+        in_specs=[smem] + [hbm] * 8,
         out_specs=(vmem, vmem),
         scratch_shapes=[
+            pltpu.VMEM((6 * NG, NG), BF16),
             pltpu.VMEM(bands.shape, BF16),
             pltpu.VMEM(slab, F32),
             pltpu.VMEM(slab, F32),
@@ -399,17 +456,17 @@
             pltpu.VMEM((16, 1, NG), F32),
             pltpu.VMEM((2, NG, NG), BF16),
             pltpu.VMEM((2, 16, KEPT, NG), BF16),
-            dma((3,)), dma((3,)), dma((3,)),
+            dma((4,)), dma((3,)), dma((3,)),
             dma(()), dma(()), dma(()), dma((16,)), dma(()), dma((ITERS,)),
             dma(()), dma(()), dma(()), dma(()), dma((2,)), dma((2,)),
         ],
         compiler_params=pltpu.CompilerParams(
-            has_side_effects=True, vmem_limit_bytes=48 * 1024 * 1024
+            has_side_effects=True, vmem_limit_bytes=67043328
         ),
         name="scf",
     )(
         occupations, bands, external, density_in, prev_density, prev_residual,
-        hist_density, hist_residual, *constants,
+        hist_density, hist_residual, jnp.asarray(tables()),
     )
 
 

time: 152 us -> 129 us (0.85)
  Pallas kernels: 140 us -> 125 us
  local copies, waits for them, and re-layouts: 10.8 us -> 3.74 us
    pallas_call x1, Pallas kernels: 140 us -> 125 us  [local(): pl.pallas_call(kernel, out_shape=(out, out), in_specs=[smem] + [hbm] * 8,...]
    unnamed x22 -> x2, local copies, waits for them, and re-layouts: 10.8 us -> 3.74 us
where the time goes in v2:
time: 129 us
  Pallas kernels  125 us (97%)
  local copies, waits for them, and re-layouts  3.74 us (3%)
    pallas_call x1, Pallas kernels, local(): pl.pallas_call(kernel, out_shape=(out, out), in_specs=[smem] + [hbm] * 8,...  125 us
    unnamed x2, local copies, waits for them, and re-layouts  3.74 us

profile of v2, /device:TPU:1, one launch (start us, length us, event | category | flops | bytes accessed | tf_op | source)
XLA Modules:
  0.0 129.0 jit_solution(11675657255708899763)
XLA Ops:
  0.6 124.6 %scf.1 = (f32[8,128,128]{2,1,0:T(8,128)}, f32[8,128,128]{2,1,0:T(8,128)}) custom-call(f32[2]{0:T(128)} %occ.1, bf16[2,2,8,128,128]{4,3,2,1,0:T(8,128)(2,1)} %bands.1, f32[8,128,128]{2,1,0:T(8,128)} %ext.1, f32[8,128,128]{2,1,0:T(8,128)} %den.1, f32[8,128,128]{2,1,0:T(8,128)} %pden.1, f32[8,128,128]{2,1,0:T(8,128)} %pres.1, f32[5,8,128,128]{3,2,1,0:T(8,128)} %hden.1, ...), custom_call_target="tpu_custom_call" | custom-call | tf_op jit(solution)/shard_map/scf/pallas_call | solution.py:429
  125.2 1.9 %copy.13 = f32[8,128,128]{2,1,0:T(8,128)} copy(f32[8,128,128]{2,1,0:T(8,128)} %get-tuple-element.4) | data formatting | bytes 1048576
  127.1 1.9 %copy.14 = f32[8,128,128]{2,1,0:T(8,128)} copy(f32[8,128,128]{2,1,0:T(8,128)} %get-tuple-element.5) | data formatting | bytes 1048576

commit v3 on v2

--- a/solution.py
+++ b/solution.py
@@ -13,6 +13,7 @@
 KEPT = NG // 2
 DEPTH = 6
 ITERS = 3
+PER = 4
 F32 = jnp.float32
 BF16 = jnp.bfloat16
 MESH = pl.DeviceIdType.MESH
@@ -56,10 +57,11 @@
     out_d, out_r,
     mats_v, bands_v, ext_v, den_v, facg, facp, plane, rs, qs, psi,
     send_f, recv_f, stage, kin, send_b, recv_b, part, recv_d, row_s, rows, occ_s, occs,
-    outs_s, outs_v,
+    outs_s,
     in_sems, pl_sems, pl_send, sf_sem, rf_sem, sb_sem, rb_sems, sd_sem, rd_sems,
     sr_sem, rr_sem, so_sem, ro_sem, sout_sems, rout_sems,
 ):
+    outs_v = (out_d, out_r)
     g = lax.axis_index("band")
     i = lax.axis_index("grid")
     core = i % 2
@@ -68,6 +70,7 @@
     zz = g % 8
     me = xy * 16 + g
     twin = i + 1 - 2 * core
+    owner = core == half
 
     def remote(src, dst, ssem, rsem, dg, di):
         return pltpu.make_async_remote_copy(
@@ -77,6 +80,48 @@
 
     def drain(ref, sem):
         pltpu.make_async_copy(ref, ref, sem).wait()
+
+    def z_of(m):
+        return (zz + 4 + (1 - 2 * (m % 2)) * ((m + 1) // 2)) % 8
+
+    def col_of(n):
+        k = n // 2
+        dx = 2 + (1 - 2 * (k % 2)) * ((k + 1) // 2)
+        return ((xy // 2 + dx) % 4) * 2 + (xy + 1 - n % 2) % 2
+
+    halves = [1 - half, half]
+    rings = [halves[h] * 8 + z_of(m) for m in range(8) for h in range(2)]
+
+    def everyone(start):
+        def column(n, carry):
+            q = col_of(n)
+            for at, dg in enumerate(rings):
+                start(dg, q, n == 7 if at == 15 else None)
+            return carry
+
+        lax.fori_loop(0, 8, column, 0)
+
+
+    barrier = pltpu.get_barrier_semaphore()
+
+    def hello(dg, di):
+        pl.semaphore_signal(barrier, inc=1, device_id=(dg, di), device_id_type=MESH)
+
+    def greet(dg, q, same):
+        if same is None:
+            hello(dg, 2 * q + core)
+        else:
+            pl.when(jnp.logical_not(same))(lambda: hello(dg, 2 * q + core))
+
+    everyone(greet)
+    for dg in rings:
+        hello(dg, twin)
+
+    def greet_column(n, carry):
+        hello(g, 2 * col_of(n) + 1 - core)
+        return carry
+
+    lax.fori_loop(0, 7, greet_column, 0)
 
     loads = [
         pltpu.make_async_copy(ext, ext_v, in_sems.at[0]),
@@ -86,30 +131,6 @@
     ]
     for load in loads:
         load.start()
-
-    owner = core == half
-
-    @pl.when(owner)
-    def _():
-        pieces = [
-            (ext.at[zz], plane.at[0], 0), (den.at[zz], plane.at[1], 0),
-            (pden.at[zz], plane.at[2], 0), (pres.at[zz], plane.at[3], 0),
-            (hden.at[:, zz], rs.at[pl.ds(0, DEPTH - 1)], 1),
-            (hres.at[:, zz], qs.at[pl.ds(0, DEPTH - 1)], 2),
-        ]
-        for src, dst, s in pieces:
-            pltpu.make_async_copy(src, dst, pl_sems.at[s]).start()
-            remote(src, dst, pl_send.at[s], pl_sems.at[s], g, twin).start()
-
-    occ_row = jnp.full((1, NG), occ[core], F32)
-    occ_s[...] = occ_row
-    occs[g] = occ_row
-
-    def send_occ(n, c):
-        remote(occ_s, occs.at[g], so_sem, ro_sem, (g + n) % 16, i).start()
-        return c
-
-    lax.fori_loop(1, 16, send_occ, 0)
 
     lane = lax.broadcasted_iota(jnp.int32, (KEPT, NG), 1)
     sgn_f = jnp.where(lane < KEPT, 1.0, -1.0).astype(F32)
@@ -121,14 +142,6 @@
         fy = (8 * xy + r - NG // 4).astype(F32)
         kin[r] = jnp.exp((fx * fx + fy * fy + fz * fz) * (-time_step / (quarter * quarter)))
 
-    def z_of(m):
-        return (zz + 4 + (1 - 2 * (m % 2)) * ((m + 1) // 2)) % 8
-
-    cols = [
-        ((xy // 2 + dx) % 4) * 2 + (xy + dy) % 2 for dx in (2, 1, 3, 0) for dy in (1, 0)
-    ]
-    halves = [1 - half, half]
-
     wzf, fcs, ics = mats_v.at[pl.ds(0, 2 * NG)], mats_v.at[pl.ds(2 * NG, NG)], mats_v.at[pl.ds(3 * NG, NG)]
     wzi = mats_v.at[pl.ds(4 * NG, NG)], mats_v.at[pl.ds(5 * NG, NG)]
 
@@ -147,8 +160,11 @@
 
     def forward_zy(w):
         a = dot(w, wzf[...]).astype(BF16)
-        b = pair_forward(jnp.concatenate([a[:NG], a[NG:]], axis=1))
-        return [v.reshape(8, 8, NG).astype(BF16) for v in b]
+        out = []
+        for at in range(0, w.shape[0], 2 * NG):
+            b = pair_forward(jnp.concatenate([a[at : at + NG], a[at + NG : at + 2 * NG]], axis=1))
+            out += [v.reshape(8, 8, NG).astype(BF16) for v in b]
+        return out
 
     def send_tile(src, dst, ssem, rsem, dg, di, same=None):
         if same is None:
@@ -174,29 +190,26 @@
                 stage[pl.ds(r + c, NG, stride=8), :] = y[:, c * NG : (c + 1) * NG]
         send_b[...] = stage[...].reshape(NG, 8, NG).astype(BF16)
 
-        def send(m, carry):
-            z = z_of(m)
-            for h in range(2):
-                dg = halves[h] * 8 + z
-                for n, q in enumerate(cols):
-                    send_tile(
-                        send_b.at[q * 16 + dg], recv_b.at[g * 8 + xy], sb_sem, rb_sems.at[g],
-                        dg, 2 * q + core, m == 7 if h == 1 and n == 7 else None,
-                    )
-            return carry
-
-        lax.fori_loop(0, 8, send, 0)
-
-    def backward(m, carry):
-        z = z_of(m)
-        ts = [halves[h] * 8 + z for h in range(2)]
+        everyone(lambda dg, q, same: send_tile(
+            send_b.at[q * 16 + dg], recv_b.at[g * 8 + xy], sb_sem, rb_sems.at[g],
+            dg, 2 * q + core, same,
+        ))
+
+    def bands_of(n):
+        return [halves[h] * 8 + z_of(n * PER + e) for e in range(PER) for h in range(2)]
+
+    def backward(n, carry):
+        ts = bands_of(n)
         d = []
         for t in ts:
             tiles = recv_b.at[pl.ds(t * 8, 8)]
             drain(tiles, rb_sems.at[t])
             d.append(tiles[...].astype(F32).reshape(KEPT, NG))
-        e = pair_inverse(d)
-        e = jnp.concatenate([e[:, :NG], e[:, NG:]], axis=0).astype(BF16)
+        e = []
+        for at in range(0, len(ts), 2):
+            both = pair_inverse(d[at : at + 2])
+            e += [both[:, :NG], both[:, NG:]]
+        e = jnp.concatenate(e, axis=0).astype(BF16)
         re = dot(e, wzi[0][...]).astype(BF16)
         im = dot(e, wzi[1][...]).astype(BF16)
         total = part[...]
@@ -216,52 +229,73 @@
                 load.wait()
             facg[...] = jnp.exp(-time_step * (ext_v[...] + den_v[...] - energy_shift))
 
-            def make_forward(which, own):
-                def forward(n, carry):
-                    w = []
-                    for c in range(2):
-                        f = facg[2 * n + c]
-                        w.append(jnp.concatenate(
-                            [bands_v[p, which, 2 * n + c].astype(F32) * f for p in range(2)], axis=1
-                        ).astype(BF16))
-                    b = forward_zy(jnp.concatenate(w, axis=0))
-                    for c in range(2):
-                        at = own * 64 + (2 * n + c) * 8
-                        send_f[pl.ds(at, 8)] = b[c]
-                        for k, q in enumerate(cols):
-                            src, dst = send_f.at[at + q], recv_f.at[8 * i + 2 * n + c]
-                            if own and k == 7:
-                                pltpu.make_async_copy(src, dst, rf_sem).start()
-                            else:
-                                send_tile(src, dst, sf_sem, rf_sem, g, 2 * q + which)
-                    return carry
-
-                return forward
-
-            lax.fori_loop(0, 4, make_forward(1 - core, 0), 0)
-            lax.fori_loop(0, 4, make_forward(core, 1), 0)
-            drain(send_f.at[pl.ds(0, 120)], sf_sem)
+            def forward(n, carry):
+                w = []
+                for c in range(2 * PER):
+                    at = n * 2 * PER + c
+                    f = facg[at % 8]
+                    w.append(jnp.concatenate(
+                        [bands_v[p, at // 8, at % 8].astype(F32) * f for p in range(2)], axis=1
+                    ).astype(BF16))
+                for c, b in enumerate(forward_zy(jnp.concatenate(w, axis=0))):
+                    send_f[pl.ds((n * 2 * PER + c) * 8, 8)] = b
+                return carry
+
+            lax.fori_loop(0, 8 // PER, forward, 0)
+            pl.semaphore_wait(barrier, 150)
+            columns = [col_of(n) for n in range(8)]
+
+            def first_sends(n, carry):
+                which, j = n // 8, n % 8
+                for k, q in enumerate(columns):
+                    send_tile(
+                        send_f.at[n * 8 + q], recv_f.at[8 * i + j], sf_sem, rf_sem, g, 2 * q + which,
+                        which == core if k == 7 else None,
+                    )
+                return carry
+
+            lax.fori_loop(0, 16, first_sends, 0)
+
+
+            @pl.when(owner)
+            def _():
+                pieces = [
+                    (ext.at[zz], plane.at[0], 0), (den.at[zz], plane.at[1], 0),
+                    (pden.at[zz], plane.at[2], 0), (pres.at[zz], plane.at[3], 0),
+                    (hden.at[:, zz], rs.at[pl.ds(0, DEPTH - 1)], 1),
+                    (hres.at[:, zz], qs.at[pl.ds(0, DEPTH - 1)], 2),
+                ]
+                for src, dst, s in pieces:
+                    pltpu.make_async_copy(src, dst, pl_sems.at[s]).start()
+                    remote(src, dst, pl_send.at[s], pl_sems.at[s], g, twin).start()
+
+            occ_row = jnp.full((1, NG), occ[core], F32)
+            occ_s[...] = occ_row
+            occs[g] = occ_row
+
+            def send_occ(n, c):
+                remote(occ_s, occs.at[g], so_sem, ro_sem, (g + n) % 16, i).start()
+                return c
+
+            lax.fori_loop(1, 16, send_occ, 0)
+
         else:
-            def forward(m, carry):
-                z = z_of(m)
+            def forward(n, carry):
+                ts = bands_of(n)
                 f = facp[...]
                 f = jnp.concatenate([f, f], axis=1)
-                ts = [halves[h] * 8 + z for h in range(2)]
                 w = jnp.concatenate([(psi[t].astype(F32) * f).astype(BF16) for t in ts], axis=0)
-                b = forward_zy(w)
-                for h, t in enumerate(ts):
-                    send_f[pl.ds(t * 8, 8)] = b[h]
-                    for n, q in enumerate(cols):
-                        send_tile(
-                            send_f.at[t * 8 + q], recv_f.at[me], sf_sem, rf_sem,
-                            t, 2 * q + core, m == 7 if h == 1 and n == 7 else None,
-                        )
+                for t, b in zip(ts, forward_zy(w)):
+                    send_f[pl.ds(t * 8, 8)] = b
                 return carry
 
-            lax.fori_loop(0, 8, forward, 0)
-            drain(send_f.at[pl.ds(0, 127)], sf_sem)
+            lax.fori_loop(0, 8 // PER, forward, 0)
+            everyone(lambda dg, q, same: send_tile(
+                send_f.at[dg * 8 + q], recv_f.at[me], sf_sem, rf_sem, dg, 2 * q + core, same,
+            ))
 
         spectral()
+        drain(send_f.at[pl.ds(0, 120 if step == 0 else 127)], sf_sem)
 
         if step == 0:
             drain(plane, pl_sems.at[0])
@@ -277,12 +311,11 @@
                 drain(qs.at[pl.ds(0, DEPTH - 1)], pl_send.at[2])
 
         part[...] = jnp.zeros_like(part)
-        lax.fori_loop(0, 8, backward, 0)
-        drain(send_b.at[pl.ds(0, 127)], sb_sem)
+        lax.fori_loop(0, 8 // PER, backward, 0)
 
         swap = remote(part, recv_d.at[step], sd_sem, rd_sems.at[step], g, twin)
         swap.start()
-        swap.wait()
+        swap.wait_recv()
         rho_out = (part[...] + recv_d[step]) * (density_scale / bands_total)
         rho_in = plane[1]
         res = rho_out - rho_in
@@ -313,20 +346,14 @@
         row_s[...] = row
         rows[me] = row
 
-        def send_row(m, carry):
-            z = z_of(m)
-            for h in range(2):
-                for n, q in enumerate(cols):
-                    copy = remote(
-                        row_s, rows.at[me], sr_sem, rr_sem, halves[h] * 8 + z, 2 * q + core
-                    )
-                    if h == 1 and n == 7:
-                        pl.when(m != 7)(copy.start)
-                    else:
-                        copy.start()
-            return carry
-
-        lax.fori_loop(0, 8, send_row, 0)
+        def send_row(dg, q, same):
+            copy = remote(row_s, rows.at[me], sr_sem, rr_sem, dg, 2 * q + core)
+            if same is None:
+                copy.start()
+            else:
+                pl.when(jnp.logical_not(same))(copy.start)
+
+        everyone(send_row)
 
         def gather(value, which):
             outs_s[which] = value.astype(BF16)
@@ -336,7 +363,7 @@
                 for h in range(2):
                     send_tile(
                         outs_s.at[which, pl.ds(pl.multiple_of(core * KEPT, KEPT), KEPT)],
-                        outs_v.at[which, 2 * zz + core], sout_sems.at[which], rout_sems.at[which],
+                        outs_v[which].at[2 * zz + core], sout_sems.at[which], rout_sems.at[which],
                         halves[h] * 8 + z, 2 * xy + half,
                         jnp.logical_and(m == 7, owner) if h == 1 else None,
                     )
@@ -347,8 +374,10 @@
         if step == ITERS - 1:
             gather(res, 1)
 
+        swap.wait_send()
         drain(rows.at[pl.ds(0, 127)], rr_sem)
         drain(rows.at[pl.ds(0, 127)], sr_sem)
+        drain(send_b.at[pl.ds(0, 127)], sb_sem)
         sums = jnp.sum(rows[...], axis=0) * (1.0 / (NG * NG * NG))
 
         def splat(at):
@@ -406,31 +435,28 @@
             facp[...] = jnp.exp(-time_step * (plane[0] + rho - energy_shift))
         else:
             gather(rho, 0)
-            for which, out in ((1, out_r), (0, out_d)):
-                drain(outs_v.at[which], rout_sems.at[which])
-                out[...] = outs_v[which].astype(F32).reshape(8, NG, NG)
+            for which in (1, 0):
+                drain(outs_v[which], rout_sems.at[which])
 
                 @pl.when(owner)
                 def _():
-                    drain(outs_v.at[which, pl.ds(0, 15)], sout_sems.at[which])
+                    drain(outs_v[which].at[pl.ds(0, 15)], sout_sems.at[which])
 
                 @pl.when(jnp.logical_not(owner))
                 def _():
-                    drain(outs_v.at[which], sout_sems.at[which])
+                    drain(outs_v[which], sout_sems.at[which])
 
 
 def local(bands, occupations, external, density_in, prev_density, prev_residual, hist_density, hist_residual):
     slab = external.shape
     hbm = pl.BlockSpec(memory_space=pltpu.HBM)
-    vmem = pl.BlockSpec(memory_space=pltpu.VMEM)
     smem = pl.BlockSpec(memory_space=pltpu.SMEM)
     dma = pltpu.SemaphoreType.DMA
-    out = jax.ShapeDtypeStruct(slab, F32)
-    return pl.pallas_call(
+    both = pl.pallas_call(
         kernel,
-        out_shape=(out, out),
+        out_shape=[jax.ShapeDtypeStruct((16, KEPT, NG), BF16)] * 2,
         in_specs=[smem] + [hbm] * 8,
-        out_specs=(vmem, vmem),
+        out_specs=[hbm] * 2,
         scratch_shapes=[
             pltpu.VMEM((6 * NG, NG), BF16),
             pltpu.VMEM(bands.shape, BF16),
@@ -455,19 +481,19 @@
             pltpu.VMEM((1, NG), F32),
             pltpu.VMEM((16, 1, NG), F32),
             pltpu.VMEM((2, NG, NG), BF16),
-            pltpu.VMEM((2, 16, KEPT, NG), BF16),
             dma((4,)), dma((3,)), dma((3,)),
             dma(()), dma(()), dma(()), dma((16,)), dma(()), dma((ITERS,)),
             dma(()), dma(()), dma(()), dma(()), dma((2,)), dma((2,)),
         ],
         compiler_params=pltpu.CompilerParams(
-            has_side_effects=True, vmem_limit_bytes=67043328
+            has_side_effects=True, collective_id=0, vmem_limit_bytes=67043328
         ),
         name="scf",
     )(
         occupations, bands, external, density_in, prev_density, prev_residual,
         hist_density, hist_residual, jnp.asarray(tables()),
     )
+    return tuple(half.reshape(slab).astype(F32) for half in both)
 
 
 def solution(mesh):

time: 129 us -> 113 us (0.88)
  Pallas kernels: 125 us -> 110 us
  local copies, waits for them, and re-layouts: 3.74 us -> 0 us
  other arithmetic: 0 us -> 2.1 us
    pallas_call x1, Pallas kernels: 125 us -> 110 us  [local(): pl.pallas_call(kernel, out_shape=[jax.ShapeDtypeStruct((16, KEPT, NG), BF...]
    unnamed x2 -> x0, local copies, waits for them, and re-layouts: 3.74 us -> none
    convert_element_type x0 -> x1, other arithmetic: none -> 2.1 us  [local(): return tuple((half.reshape(slab).astype(F32) for half in both))]
where the time goes in v3:
time: 113 us
  Pallas kernels  110 us (97%)
  other arithmetic  2.1 us (2%)
    pallas_call x1, Pallas kernels, local(): pl.pallas_call(kernel, out_shape=[jax.ShapeDtypeStruct((16, KEPT, NG), BF...  110 us

profile of v3, /device:TPU:1, one launch (start us, length us, event | category | flops | bytes accessed | tf_op | source)
XLA Modules:
  0.0 112.7 jit_solution(811005074373317689)
XLA Ops:
  0.6 110.0 %scf.1 = (bf16[16,64,128]{2,1,0:T(8,128)(2,1)}, bf16[16,64,128]{2,1,0:T(8,128)(2,1)}) custom-call(f32[2]{0:T(128)} %occ.1, bf16[2,2,8,128,128]{4,3,2,1,0:T(8,128)(2,1)} %bands.1, f32[8,128,128]{2,1,0:T(8,128)} %ext.1, f32[8,128,128]{2,1,0:T(8,128)} %den.1, f32[8,128,128]{2,1,0:T(8,128)} %pden.1, f32[8,128,128]{2,1,0:T(8,128)} %pres.1, ...), custom_call_target="tpu_custom_call" | custom-call | tf_op jit(solution)/shard_map/scf/pallas_call | solution.py:455
  110.6 2.1 %bitcast_convert_fusion = (f32[8,128,128]{2,1,0:T(8,128)}, f32[8,128,128]{2,1,0:T(8,128)}) fusion(bf16[8,128,128]{2,1,0:T(8,128)(2,1)} %bitcast.8, bf16[8,128,128]{2,1,0:T(8,128)(2,1)} %bitcast.7), kind=kLoop, calls=%fused_computation | loop fusion | flops 262144 | bytes 1572864 | tf_op jit(solution)/shard_map/convert_element_type | solution.py:496

commit v4 on v3

--- a/solution.py
+++ b/solution.py
@@ -57,11 +57,10 @@
     out_d, out_r,
     mats_v, bands_v, ext_v, den_v, facg, facp, plane, rs, qs, psi,
     send_f, recv_f, stage, kin, send_b, recv_b, part, recv_d, row_s, rows, occ_s, occs,
-    outs_s,
+    outs_s, res_v, den_s, rslab, qslab, pden_v, pres_v, coef_v,
     in_sems, pl_sems, pl_send, sf_sem, rf_sem, sb_sem, rb_sems, sd_sem, rd_sems,
-    sr_sem, rr_sem, so_sem, ro_sem, sout_sems, rout_sems,
+    sr_sem, rr_sem, so_sem, ro_sem, sout_sems, rout_sems, late_sems, fin_sems,
 ):
-    outs_v = (out_d, out_r)
     g = lax.axis_index("band")
     i = lax.axis_index("grid")
     core = i % 2
@@ -81,48 +80,6 @@
     def drain(ref, sem):
         pltpu.make_async_copy(ref, ref, sem).wait()
 
-    def z_of(m):
-        return (zz + 4 + (1 - 2 * (m % 2)) * ((m + 1) // 2)) % 8
-
-    def col_of(n):
-        k = n // 2
-        dx = 2 + (1 - 2 * (k % 2)) * ((k + 1) // 2)
-        return ((xy // 2 + dx) % 4) * 2 + (xy + 1 - n % 2) % 2
-
-    halves = [1 - half, half]
-    rings = [halves[h] * 8 + z_of(m) for m in range(8) for h in range(2)]
-
-    def everyone(start):
-        def column(n, carry):
-            q = col_of(n)
-            for at, dg in enumerate(rings):
-                start(dg, q, n == 7 if at == 15 else None)
-            return carry
-
-        lax.fori_loop(0, 8, column, 0)
-
-
-    barrier = pltpu.get_barrier_semaphore()
-
-    def hello(dg, di):
-        pl.semaphore_signal(barrier, inc=1, device_id=(dg, di), device_id_type=MESH)
-
-    def greet(dg, q, same):
-        if same is None:
-            hello(dg, 2 * q + core)
-        else:
-            pl.when(jnp.logical_not(same))(lambda: hello(dg, 2 * q + core))
-
-    everyone(greet)
-    for dg in rings:
-        hello(dg, twin)
-
-    def greet_column(n, carry):
-        hello(g, 2 * col_of(n) + 1 - core)
-        return carry
-
-    lax.fori_loop(0, 7, greet_column, 0)
-
     loads = [
         pltpu.make_async_copy(ext, ext_v, in_sems.at[0]),
         pltpu.make_async_copy(den, den_v, in_sems.at[1]),
@@ -131,6 +88,54 @@
     ]
     for load in loads:
         load.start()
+    late = [
+        pltpu.make_async_copy(hden, rslab.at[pl.ds(0, DEPTH - 1)], late_sems.at[0]),
+        pltpu.make_async_copy(hres, qslab.at[pl.ds(0, DEPTH - 1)], late_sems.at[1]),
+        pltpu.make_async_copy(pden, pden_v, late_sems.at[2]),
+        pltpu.make_async_copy(pres, pres_v, late_sems.at[3]),
+    ]
+
+    def z_of(m):
+        return (zz + 4 + (1 - 2 * (m % 2)) * ((m + 1) // 2)) % 8
+
+    def col_of(n):
+        k = n // 2
+        dx = 2 + (1 - 2 * (k % 2)) * ((k + 1) // 2)
+        return ((xy // 2 + dx) % 4) * 2 + (xy + 1 - n % 2) % 2
+
+    halves = [1 - half, half]
+    rings = [halves[h] * 8 + z_of(m) for m in range(8) for h in range(2)]
+
+    def everyone(start):
+        def column(n, carry):
+            q = col_of(n)
+            for at, dg in enumerate(rings):
+                start(dg, q, n == 7 if at == 15 else None)
+            return carry
+
+        lax.fori_loop(0, 8, column, 0)
+
+
+    barrier = pltpu.get_barrier_semaphore()
+
+    def hello(dg, di):
+        pl.semaphore_signal(barrier, inc=1, device_id=(dg, di), device_id_type=MESH)
+
+    def greet(dg, q, same):
+        if same is None:
+            hello(dg, 2 * q + core)
+        else:
+            pl.when(jnp.logical_not(same))(lambda: hello(dg, 2 * q + core))
+
+    everyone(greet)
+    for dg in rings:
+        hello(dg, twin)
+
+    def greet_column(n, carry):
+        hello(g, 2 * col_of(n) + 1 - core)
+        return carry
+
+    lax.fori_loop(0, 7, greet_column, 0)
 
     lane = lax.broadcasted_iota(jnp.int32, (KEPT, NG), 1)
     sgn_f = jnp.where(lane < KEPT, 1.0, -1.0).astype(F32)
@@ -222,6 +227,43 @@
         part[...] = total
         return carry
 
+    def rows_of(a):
+        return a.reshape(16, 8, NG)
+
+    def slab_update(done):
+        drain(res_v.at[done], rout_sems.at[done])
+        last = done == ITERS - 1
+        if last:
+            keep = pltpu.make_async_copy(res_v.at[done], out_r, fin_sems.at[1])
+            keep.start()
+
+        def one_plane(j, carry):
+            here = res_v[done, pl.ds(2 * j, 2)].astype(F32).reshape(NG, NG)
+            inside = den_v[j]
+            fresh_r, fresh_q = inside - pden_v[j], here - pres_v[j]
+            mixed = rows_of(inside + mixing_weight * here)
+            for k in range(DEPTH):
+                r = rslab[done + k, j] if k < DEPTH - 1 else fresh_r
+                q = qslab[done + k, j] if k < DEPTH - 1 else fresh_q
+                mixed = mixed - coef_v[done, k][None] * rows_of(r + mixing_weight * q)
+            mixed = mixed.reshape(NG, NG)
+            if last:
+                den_s[pl.ds(2 * j, 2)] = mixed.reshape(2, KEPT, NG).astype(BF16)
+            else:
+                rslab[DEPTH - 1 + done, j] = fresh_r
+                qslab[DEPTH - 1 + done, j] = fresh_q
+                pden_v[j] = inside
+                pres_v[j] = here
+                den_v[j] = mixed
+            return carry
+
+        lax.fori_loop(0, 8, one_plane, 0)
+        if last:
+            leave = pltpu.make_async_copy(den_s, out_d, fin_sems.at[0])
+            leave.start()
+            leave.wait()
+            keep.wait()
+
     gram = None
     for step in range(ITERS):
         if step == 0:
@@ -255,6 +297,8 @@
                 return carry
 
             lax.fori_loop(0, 16, first_sends, 0)
+            for copy in late:
+                copy.start()
 
 
             @pl.when(owner)
@@ -294,6 +338,11 @@
                 send_f.at[dg * 8 + q], recv_f.at[me], sf_sem, rf_sem, dg, 2 * q + core, same,
             ))
 
+        if step:
+            if step == 1:
+                for copy in late:
+                    copy.wait()
+            slab_update(step - 1)
         spectral()
         drain(send_f.at[pl.ds(0, 120 if step == 0 else 127)], sf_sem)
 
@@ -322,9 +371,6 @@
         newest = res - plane[3]
         rs[DEPTH - 1 + step] = rho_in - plane[2]
         qs[DEPTH - 1 + step] = newest
-
-        def rows_of(a):
-            return a.reshape(16, 8, NG)
 
         lanes = lax.broadcasted_iota(jnp.int32, (1, NG), 1)
         row = jnp.zeros((1, NG), F32)
@@ -355,24 +401,20 @@
 
         everyone(send_row)
 
-        def gather(value, which):
-            outs_s[which] = value.astype(BF16)
-
-            def send(m, carry):
-                z = z_of(m)
-                for h in range(2):
-                    send_tile(
-                        outs_s.at[which, pl.ds(pl.multiple_of(core * KEPT, KEPT), KEPT)],
-                        outs_v[which].at[2 * zz + core], sout_sems.at[which], rout_sems.at[which],
-                        halves[h] * 8 + z, 2 * xy + half,
-                        jnp.logical_and(m == 7, owner) if h == 1 else None,
-                    )
-                return carry
-
-            lax.fori_loop(0, 8, send, 0)
-
-        if step == ITERS - 1:
-            gather(res, 1)
+        outs_s[step] = res.astype(BF16)
+
+        def send_res(m, carry):
+            z = z_of(m)
+            for h in range(2):
+                send_tile(
+                    outs_s.at[step, pl.ds(pl.multiple_of(core * KEPT, KEPT), KEPT)],
+                    res_v.at[step, 2 * zz + core], sout_sems.at[step], rout_sems.at[step],
+                    halves[h] * 8 + z, 2 * xy + half,
+                    jnp.logical_and(m == 7, owner) if h == 1 else None,
+                )
+            return carry
+
+        lax.fori_loop(0, 8, send_res, 0)
 
         swap.wait_send()
         drain(rows.at[pl.ds(0, 127)], rr_sem)
@@ -424,27 +466,28 @@
             for k in range(r + 1, DEPTH):
                 value = value - low[k][r] * coeffs[k]
             coeffs[r] = value
+        for k in range(DEPTH):
+            coef_v[step, k] = coeffs[k]
+        if step == ITERS - 1:
+            break
         mixed = rows_of(rho_in + mixing_weight * res)
         for j in range(DEPTH):
             mixed = mixed - coeffs[j][None] * rows_of(rs[step + j] + mixing_weight * qs[step + j])
         rho = mixed.reshape(NG, NG)
-        if step < ITERS - 1:
-            plane[2] = rho_in
-            plane[3] = res
-            plane[1] = rho
-            facp[...] = jnp.exp(-time_step * (plane[0] + rho - energy_shift))
-        else:
-            gather(rho, 0)
-            for which in (1, 0):
-                drain(outs_v[which], rout_sems.at[which])
-
-                @pl.when(owner)
-                def _():
-                    drain(outs_v[which].at[pl.ds(0, 15)], sout_sems.at[which])
-
-                @pl.when(jnp.logical_not(owner))
-                def _():
-                    drain(outs_v[which], sout_sems.at[which])
+        plane[2] = rho_in
+        plane[3] = res
+        plane[1] = rho
+        facp[...] = jnp.exp(-time_step * (plane[0] + rho - energy_shift))
+
+    slab_update(ITERS - 1)
+    for step in range(ITERS):
+        @pl.when(owner)
+        def _():
+            drain(res_v.at[step, pl.ds(0, 15)], sout_sems.at[step])
+
+        @pl.when(jnp.logical_not(owner))
+        def _():
+            drain(res_v.at[step], sout_sems.at[step])
 
 
 def local(bands, occupations, external, density_in, prev_density, prev_residual, hist_density, hist_residual):
@@ -480,10 +523,17 @@
             pltpu.VMEM((128, 1, NG), F32),
             pltpu.VMEM((1, NG), F32),
             pltpu.VMEM((16, 1, NG), F32),
-            pltpu.VMEM((2, NG, NG), BF16),
+            pltpu.VMEM((ITERS, NG, NG), BF16),
+            pltpu.VMEM((ITERS, 16, KEPT, NG), BF16),
+            pltpu.VMEM((16, KEPT, NG), BF16),
+            pltpu.VMEM((DEPTH - 1 + ITERS, *slab), F32),
+            pltpu.VMEM((DEPTH - 1 + ITERS, *slab), F32),
+            pltpu.VMEM(slab, F32),
+            pltpu.VMEM(slab, F32),
+            pltpu.VMEM((ITERS, DEPTH, 8, NG), F32),
             dma((4,)), dma((3,)), dma((3,)),
             dma(()), dma(()), dma(()), dma((16,)), dma(()), dma((ITERS,)),
-            dma(()), dma(()), dma(()), dma(()), dma((2,)), dma((2,)),
+            dma(()), dma(()), dma(()), dma(()), dma((ITERS,)), dma((ITERS,)), dma((4,)), dma((2,)),
         ],
         compiler_params=pltpu.CompilerParams(
             has_side_effects=True, collective_id=0, vmem_limit_bytes=67043328

time: 113 us -> 108 us (0.956)
  Pallas kernels: 110 us -> 105 us
    pallas_call x1, Pallas kernels: 110 us -> 105 us  [local(): pl.pallas_call(kernel, out_shape=[jax.ShapeDtypeStruct((16, KEPT, NG), BF...]
where the time goes in v4:
time: 108 us; the launch traced here: 107 us
  Pallas kernels  105 us (97%)
  other arithmetic  2.1 us (2%)
    pallas_call x1, Pallas kernels, local(): pl.pallas_call(kernel, out_shape=[jax.ShapeDtypeStruct((16, KEPT, NG), BF...  105 us

profile of v4, /device:TPU:1, one launch (start us, length us, event | category | flops | bytes accessed | tf_op | source)
XLA Modules:
  0.0 107.5 jit_solution(4568604662554816763)
XLA Ops:
  0.6 104.7 %scf.1 = (bf16[16,64,128]{2,1,0:T(8,128)(2,1)}, bf16[16,64,128]{2,1,0:T(8,128)(2,1)}) custom-call(f32[2]{0:T(128)} %occ.1, bf16[2,2,8,128,128]{4,3,2,1,0:T(8,128)(2,1)} %bands.1, f32[8,128,128]{2,1,0:T(8,128)} %ext.1, f32[8,128,128]{2,1,0:T(8,128)} %den.1, f32[8,128,128]{2,1,0:T(8,128)} %pden.1, f32[8,128,128]{2,1,0:T(8,128)} %pres.1, ...), custom_call_target="tpu_custom_call" | custom-call | tf_op jit(solution)/shard_map/scf/pallas_call | solution.py:498
  105.4 2.1 %bitcast_convert_fusion = (f32[8,128,128]{2,1,0:T(8,128)}, f32[8,128,128]{2,1,0:T(8,128)}) fusion(bf16[8,128,128]{2,1,0:T(8,128)(2,1)} %bitcast.8, bf16[8,128,128]{2,1,0:T(8,128)(2,1)} %bitcast.7), kind=kLoop, calls=%fused_computation | loop fusion | flops 262144 | bytes 1572864 | tf_op jit(solution)/shard_map/convert_element_type | solution.py:546

commit v5 on v4

--- a/solution.py
+++ b/solution.py
@@ -13,7 +13,8 @@
 KEPT = NG // 2
 DEPTH = 6
 ITERS = 3
-PER = 4
+PF = 4
+PB = 4
 F32 = jnp.float32
 BF16 = jnp.bfloat16
 MESH = pl.DeviceIdType.MESH
@@ -115,6 +116,17 @@
 
         lax.fori_loop(0, 8, column, 0)
 
+    columns = [col_of(n) for n in range(8)]
+
+    def hops(n, at):
+        dx, dz = (2, 1, 1, 0)[n // 2], (4, 3, 3, 2, 2, 1, 1, 0)[at // 2]
+        return dx + dz + (2 * (1 - n % 2) if at % 2 else 1)
+
+    far_first = sorted(
+        [(n, at) for n in range(8) for at in range(16) if (n, at) != (7, 15)],
+        key=lambda p: -hops(*p),
+    )
+
 
     barrier = pltpu.get_barrier_semaphore()
 
@@ -195,16 +207,19 @@
                 stage[pl.ds(r + c, NG, stride=8), :] = y[:, c * NG : (c + 1) * NG]
         send_b[...] = stage[...].reshape(NG, 8, NG).astype(BF16)
 
-        everyone(lambda dg, q, same: send_tile(
-            send_b.at[q * 16 + dg], recv_b.at[g * 8 + xy], sb_sem, rb_sems.at[g],
-            dg, 2 * q + core, same,
-        ))
-
-    def bands_of(n):
-        return [halves[h] * 8 + z_of(n * PER + e) for e in range(PER) for h in range(2)]
+        pltpu.make_async_copy(send_b.at[me], recv_b.at[g * 8 + xy], rb_sems.at[g]).start()
+        for n, at in far_first:
+            q, dg = columns[n], rings[at]
+            send_tile(
+                send_b.at[q * 16 + dg], recv_b.at[g * 8 + xy], sb_sem, rb_sems.at[g],
+                dg, 2 * q + core,
+            )
+
+    def bands_of(n, per):
+        return [halves[h] * 8 + z_of(n * per + e) for e in range(per) for h in range(2)]
 
     def backward(n, carry):
-        ts = bands_of(n)
+        ts = bands_of(n, PB)
         d = []
         for t in ts:
             tiles = recv_b.at[pl.ds(t * 8, 8)]
@@ -243,12 +258,19 @@
             fresh_r, fresh_q = inside - pden_v[j], here - pres_v[j]
             mixed = rows_of(inside + mixing_weight * here)
             for k in range(DEPTH):
-                r = rslab[done + k, j] if k < DEPTH - 1 else fresh_r
-                q = qslab[done + k, j] if k < DEPTH - 1 else fresh_q
-                mixed = mixed - coef_v[done, k][None] * rows_of(r + mixing_weight * q)
+                if k == DEPTH - 1:
+                    move = fresh_r + mixing_weight * fresh_q
+                elif last:
+                    move = rslab[done + k, j]
+                else:
+                    move = rslab[done + k, j] + mixing_weight * qslab[done + k, j]
+                mixed = mixed - coef_v[done, k][None] * rows_of(move)
             mixed = mixed.reshape(NG, NG)
             if last:
                 den_s[pl.ds(2 * j, 2)] = mixed.reshape(2, KEPT, NG).astype(BF16)
+                pltpu.make_async_copy(
+                    den_s.at[pl.ds(2 * j, 2)], out_d.at[pl.ds(2 * j, 2)], fin_sems.at[0]
+                ).start()
             else:
                 rslab[DEPTH - 1 + done, j] = fresh_r
                 qslab[DEPTH - 1 + done, j] = fresh_q
@@ -259,9 +281,7 @@
 
         lax.fori_loop(0, 8, one_plane, 0)
         if last:
-            leave = pltpu.make_async_copy(den_s, out_d, fin_sems.at[0])
-            leave.start()
-            leave.wait()
+            pltpu.make_async_copy(den_s, out_d, fin_sems.at[0]).wait()
             keep.wait()
 
     gram = None
@@ -273,19 +293,18 @@
 
             def forward(n, carry):
                 w = []
-                for c in range(2 * PER):
-                    at = n * 2 * PER + c
+                for c in range(2 * PF):
+                    at = n * 2 * PF + c
                     f = facg[at % 8]
                     w.append(jnp.concatenate(
                         [bands_v[p, at // 8, at % 8].astype(F32) * f for p in range(2)], axis=1
                     ).astype(BF16))
                 for c, b in enumerate(forward_zy(jnp.concatenate(w, axis=0))):
-                    send_f[pl.ds((n * 2 * PER + c) * 8, 8)] = b
+                    send_f[pl.ds((n * 2 * PF + c) * 8, 8)] = b
                 return carry
 
-            lax.fori_loop(0, 8 // PER, forward, 0)
+            lax.fori_loop(0, 8 // PF, forward, 0)
             pl.semaphore_wait(barrier, 150)
-            columns = [col_of(n) for n in range(8)]
 
             def first_sends(n, carry):
                 which, j = n // 8, n % 8
@@ -325,7 +344,7 @@
 
         else:
             def forward(n, carry):
-                ts = bands_of(n)
+                ts = bands_of(n, PF)
                 f = facp[...]
                 f = jnp.concatenate([f, f], axis=1)
                 w = jnp.concatenate([(psi[t].astype(F32) * f).astype(BF16) for t in ts], axis=0)
@@ -333,10 +352,13 @@
                     send_f[pl.ds(t * 8, 8)] = b
                 return carry
 
-            lax.fori_loop(0, 8 // PER, forward, 0)
-            everyone(lambda dg, q, same: send_tile(
-                send_f.at[dg * 8 + q], recv_f.at[me], sf_sem, rf_sem, dg, 2 * q + core, same,
-            ))
+            lax.fori_loop(0, 8 // PF, forward, 0)
+            pltpu.make_async_copy(send_f.at[g * 8 + xy], recv_f.at[me], rf_sem).start()
+            for n, at in far_first:
+                q, dg = columns[n], rings[at]
+                send_tile(
+                    send_f.at[dg * 8 + q], recv_f.at[me], sf_sem, rf_sem, dg, 2 * q + core
+                )
 
         if step:
             if step == 1:
@@ -360,7 +382,7 @@
                 drain(qs.at[pl.ds(0, DEPTH - 1)], pl_send.at[2])
 
         part[...] = jnp.zeros_like(part)
-        lax.fori_loop(0, 8 // PER, backward, 0)
+        lax.fori_loop(0, 8 // PB, backward, 0)
 
         swap = remote(part, recv_d.at[step], sd_sem, rd_sems.at[step], g, twin)
         swap.start()
@@ -392,14 +414,10 @@
         row_s[...] = row
         rows[me] = row
 
-        def send_row(dg, q, same):
-            copy = remote(row_s, rows.at[me], sr_sem, rr_sem, dg, 2 * q + core)
-            if same is None:
-                copy.start()
-            else:
-                pl.when(jnp.logical_not(same))(copy.start)
-
-        everyone(send_row)
+        for n, at in far_first:
+            remote(
+                row_s, rows.at[me], sr_sem, rr_sem, rings[at], 2 * columns[n] + core
+            ).start()
 
         outs_s[step] = res.astype(BF16)
 
@@ -415,6 +433,14 @@
             return carry
 
         lax.fori_loop(0, 8, send_res, 0)
+
+        if step == ITERS - 1:
+            def join(j, carry):
+                for k in range(step, step + DEPTH - 1):
+                    rslab[k, j] = rslab[k, j] + mixing_weight * qslab[k, j]
+                return carry
+
+            lax.fori_loop(0, 8, join, 0)
 
         swap.wait_send()
         drain(rows.at[pl.ds(0, 127)], rr_sem)

time: 108 us -> 104 us (0.963)
  Pallas kernels: 105 us -> 101 us
    pallas_call x1, Pallas kernels: 105 us -> 101 us  [local(): pl.pallas_call(kernel, out_shape=[jax.ShapeDtypeStruct((16, KEPT, NG), BF...]
where the time goes in v5:
time: 104 us
  Pallas kernels  101 us (97%)
  other arithmetic  2.1 us (2%)
    pallas_call x1, Pallas kernels, local(): pl.pallas_call(kernel, out_shape=[jax.ShapeDtypeStruct((16, KEPT, NG), BF...  101 us
    convert_element_type x1, other arithmetic, local(): return tuple((half.reshape(slab).astype(F32) for half in both))  2.1 us

profile of v5, /device:TPU:1, one launch (start us, length us, event | category | flops | bytes accessed | tf_op | source)
XLA Modules:
  0.0 103.9 jit_solution(5608670767292773954)
XLA Ops:
  0.6 101.1 %scf.1 = (bf16[16,64,128]{2,1,0:T(8,128)(2,1)}, bf16[16,64,128]{2,1,0:T(8,128)(2,1)}) custom-call(f32[2]{0:T(128)} %occ.1, bf16[2,2,8,128,128]{4,3,2,1,0:T(8,128)(2,1)} %bands.1, f32[8,128,128]{2,1,0:T(8,128)} %ext.1, f32[8,128,128]{2,1,0:T(8,128)} %den.1, f32[8,128,128]{2,1,0:T(8,128)} %pden.1, f32[8,128,128]{2,1,0:T(8,128)} %pres.1, ...), custom_call_target="tpu_custom_call" | custom-call | tf_op jit(solution)/shard_map/scf/pallas_call | solution.py:524
  101.8 2.1 %bitcast_convert_fusion = (f32[8,128,128]{2,1,0:T(8,128)}, f32[8,128,128]{2,1,0:T(8,128)}) fusion(bf16[8,128,128]{2,1,0:T(8,128)(2,1)} %bitcast.8, bf16[8,128,128]{2,1,0:T(8,128)(2,1)} %bitcast.7), kind=kLoop, calls=%fused_computation | loop fusion | flops 262144 | bytes 1572864 | tf_op jit(solution)/shard_map/convert_element_type | solution.py:572

commit v6 on v5

--- a/solution.py
+++ b/solution.py
@@ -1,3 +1,4 @@
+import functools
 import math
 
 import jax
@@ -218,7 +219,7 @@
     def bands_of(n, per):
         return [halves[h] * 8 + z_of(n * per + e) for e in range(per) for h in range(2)]
 
-    def backward(n, carry):
+    def backward(n, carry, keep=True):
         ts = bands_of(n, PB)
         d = []
         for t in ts:
@@ -235,8 +236,9 @@
         total = part[...]
         for h, t in enumerate(ts):
             mine = slice(h * NG, (h + 1) * NG)
-            psi[t, :, :NG] = re[mine]
-            psi[t, :, NG:] = im[mine]
+            if keep:
+                psi[t, :, :NG] = re[mine]
+                psi[t, :, NG:] = im[mine]
             wide_re, wide_im = re[mine].astype(F32), im[mine].astype(F32)
             total = total + occs[t] * (wide_re * wide_re + wide_im * wide_im)
         part[...] = total
@@ -381,8 +383,22 @@
                 drain(rs.at[pl.ds(0, DEPTH - 1)], pl_send.at[1])
                 drain(qs.at[pl.ds(0, DEPTH - 1)], pl_send.at[2])
 
+        lanes = lax.broadcasted_iota(jnp.int32, (1, NG), 1)
+        row = jnp.zeros((1, NG), F32)
+
+        def put(row, at, a, b):
+            total = jnp.sum(jnp.sum(rows_of(a * b), axis=0), axis=0, keepdims=True)
+            return jnp.where(lanes == at, jnp.sum(total, axis=1, keepdims=True), row)
+
+        if step == 0:
+            at = 2 * DEPTH
+            for a in range(DEPTH - 1):
+                for b in range(a + 1):
+                    row = put(row, at, qs[a], qs[b])
+                    at += 1
+
         part[...] = jnp.zeros_like(part)
-        lax.fori_loop(0, 8 // PB, backward, 0)
+        lax.fori_loop(0, 8 // PB, functools.partial(backward, keep=step < ITERS - 1), 0)
 
         swap = remote(part, recv_d.at[step], sd_sem, rd_sems.at[step], g, twin)
         swap.start()
@@ -394,23 +410,10 @@
         rs[DEPTH - 1 + step] = rho_in - plane[2]
         qs[DEPTH - 1 + step] = newest
 
-        lanes = lax.broadcasted_iota(jnp.int32, (1, NG), 1)
-        row = jnp.zeros((1, NG), F32)
-
-        def put(row, at, a, b):
-            total = jnp.sum(jnp.sum(rows_of(a * b), axis=0), axis=0, keepdims=True)
-            return jnp.where(lanes == at, jnp.sum(total, axis=1, keepdims=True), row)
-
         for j in range(DEPTH):
             q = qs[step + j]
             row = put(row, j, q, newest)
             row = put(row, DEPTH + j, q, res)
-        if step == 0:
-            at = 2 * DEPTH
-            for a in range(DEPTH - 1):
-                for b in range(a + 1):
-                    row = put(row, at, qs[a], qs[b])
-                    at += 1
         row_s[...] = row
         rows[me] = row
 

time: 104 us -> 104 us (level)
  no operation moved by 1% of the time
where the time goes in v6:
time: 104 us
  Pallas kernels  101 us (97%)
  other arithmetic  2.1 us (2%)
    pallas_call x1, Pallas kernels, local(): pl.pallas_call(kernel, out_shape=[jax.ShapeDtypeStruct((16, KEPT, NG), BF...  101 us
    convert_element_type x1, other arithmetic, local(): return tuple((half.reshape(slab).astype(F32) for half in both))  2.1 us

profile of v6, /device:TPU:1, one launch (start us, length us, event | category | flops | bytes accessed | tf_op | source)
XLA Modules:
  0.0 103.7 jit_solution(4780780196702737211)
XLA Ops:
  0.6 101.0 %scf.1 = (bf16[16,64,128]{2,1,0:T(8,128)(2,1)}, bf16[16,64,128]{2,1,0:T(8,128)(2,1)}) custom-call(f32[2]{0:T(128)} %occ.1, bf16[2,2,8,128,128]{4,3,2,1,0:T(8,128)(2,1)} %bands.1, f32[8,128,128]{2,1,0:T(8,128)} %ext.1, f32[8,128,128]{2,1,0:T(8,128)} %den.1, f32[8,128,128]{2,1,0:T(8,128)} %pden.1, f32[8,128,128]{2,1,0:T(8,128)} %pres.1, ...), custom_call_target="tpu_custom_call" | custom-call | tf_op jit(solution)/shard_map/scf/pallas_call | solution.py:527
  101.6 2.1 %bitcast_convert_fusion = (f32[8,128,128]{2,1,0:T(8,128)}, f32[8,128,128]{2,1,0:T(8,128)}) fusion(bf16[8,128,128]{2,1,0:T(8,128)(2,1)} %bitcast.8, bf16[8,128,128]{2,1,0:T(8,128)(2,1)} %bitcast.7), kind=kLoop, calls=%fused_computation | loop fusion | flops 262144 | bytes 1572864 | tf_op jit(solution)/shard_map/convert_element_type | solution.py:575
